TPU v7x, 128 devices: a whole 4x4x4 slice. The times are simulated.
128 devices in a mesh: seq: 8 (over z, core), head: 16 (over x, y).
Axes of the slice: x: 4, y: 4, z: 4, core: 2. Of those that a mesh axis runs over, the one named last changes fastest.
Arguments:
- lengths: int32 [16], replicated, may hold values from 128 to 8192, as said below
- page_owner: int32 [1536], replicated, may hold values from 0 to 16, as said below
- page_index: int32 [1536], replicated, may hold values from 0 to 127, as said below
- page_dest: int32 [1536], replicated, may hold values from 0 to 1535, as said below
- src_cache: bfloat16 [1536, 8, 64, 256], P(('seq', 'head')), may hold values from -8 to 8
- queries: bfloat16 [2, 16, 4096], replicated, may hold values from -8 to 8
- new_kv: bfloat16 [2, 16, 8, 256], replicated, may hold values from -6 to 6
- hidden_in: bfloat16 [2, 16, 4096], P(None, None, ('seq', 'head')), may hold values from -60 to 60
- out_weight: bfloat16 [4096, 4096], P(None, ('seq', 'head')), may hold values from -1.5 to 1.5
- norm_gain: bfloat16 [4096], P(('seq', 'head')), may hold values from 0.099609375 to 1.8984375
- router: bfloat16 [4096, 8], P(('seq', 'head')), may hold values from -0.09375 to 0.09375
- routes: int32 [2, 16, 2], replicated, may hold values from 0 to 7, all different within a row
- w_gate: bfloat16 [8, 4096, 8192], P('seq', None, 'head'), may hold values from -0.09375 to 0.09375
- w_up: bfloat16 [8, 4096, 8192], P('seq', None, 'head'), may hold values from -0.09375 to 0.09375
- w_down: bfloat16 [8, 8192, 4096], P('seq', 'head'), may hold values from -0.0625 to 0.0625
Outputs:
- page_pool: bfloat16 [16, 768, 64, 256], P('head', 'seq')
- mixed: bfloat16 [2, 16, 4096], P(None, None, ('seq', 'head'))
Inputs may be any that keep to these rules, and one draw needn't show every extreme that they name: Each length is at least 128; one equals 8192; the requests' pages, lengths[r] / 64 rounded up for request r, fit into the 1536 pages. `page_owner`: request r owns exactly lengths[r] / 64 rounded up source pages; the other pages carry 16. `page_index`: the pages of request r carry 0 to their count minus 1, each once; pages without request carry 0. `page_dest`: A permutation. Slot g belongs to destination group ((g % 768) // 96) * 2 + g // 768. Of the 12 pages that one device holds (pages i * 12 to (i + 1) * 12 - 1), at most 1 go to one group, and every draw has a device that sends exactly 1 to some group.
All inputs are finite; a program needn't handle non-finite values.
Results may differ from a plain program's by a relative error of at most 0.009.
Values may be sent and summed in bfloat16 or wider, within the bound.
A program may use at most 128 MiB of HBM per device.

v0:
```python
import jax
import jax.numpy as jnp
from jax import lax
from jax.sharding import Mesh
from jax.sharding import PartitionSpec as P

D = 4096
HQ = 32
KVH = 8
HD = 128
TOPK = 2
PAGE = 64
REQS = 16
SEQ = ("seq_0", "seq_1")
HEAD = ("head_0", "head_1")
SEQ_HEAD = ("seq_0", "seq_1", "head_0", "head_1")


NEG_FILL = -1e30
EPSILON = 1e-05
HIGHEST = lax.Precision.HIGHEST


def joined_all(array, axes, combine):
    for axis in axes:
        pieces = jax.tree.map(lambda part: lax.all_gather(part, axis), array)
        array = jax.tree.map(lambda part: part[0], pieces)
        for k in range(1, lax.axis_size(axis)):
            array = combine(array, jax.tree.map(lambda part: part[k], pieces))
    return array


def over_axes(array, axes):
    for axis in axes:
        array = lax.psum(array, axis)
    return array


def in_blocks(array, dim, peers):
    lengths = array.shape
    blocks = array.reshape(*lengths[:dim], peers, lengths[dim] // peers, *lengths[dim + 1 :])
    return jnp.moveaxis(blocks, dim, 0)


def cut_rows(length, count):
    unit = 8 if length >= 8 * count else 1
    return [length // unit * k // count * unit for k in range(1, count)]


def own_block(blocks, axes, sequence):
    lengths = [lax.axis_size(a) for a in axes]
    blocks = blocks.reshape(*lengths, *blocks.shape[1:])
    blocks = blocks.transpose(*sequence, *range(len(axes), blocks.ndim))
    blocks = blocks.reshape(-1, *blocks.shape[len(axes) :])
    for k in sequence:
        blocks = lax.psum_scatter(blocks, axes[k], scatter_dimension=0, tiled=True)
    return blocks[0]


def sum_all_axes_2(array, axes, dim):
    blocks = in_blocks(array, dim, lax.axis_size(axes))
    widest = max(range(1, max(2, blocks.ndim - 1)), key=lambda d: blocks.shape[d])
    count, gathered = (len(axes), [])
    for initial, share in enumerate(
        jnp.split(blocks, cut_rows(blocks.shape[widest], count), axis=widest)
    ):
        if share.size:
            sequence = [(initial + k) % count for k in range(count)]
            gathered.append(own_block(share, axes, sequence))
    return jnp.concatenate(gathered, axis=widest - 1)


def gate_mix(logits, picked):
    expert_ids = jnp.arange(logits.shape[1], dtype=jnp.int32)[None, :]
    first_hit = picked[:, 0:1] == expert_ids
    second_hit = picked[:, 1:2] == expert_ids
    first_logit = jnp.sum(jnp.where(first_hit, logits, 0.0), axis=1)
    second_logit = jnp.sum(jnp.where(second_hit, logits, 0.0), axis=1)
    leading = 1.0 / (1.0 + jnp.exp(second_logit - first_logit))
    trailing = 1.0 / (1.0 + jnp.exp(first_logit - second_logit))
    return jnp.where(first_hit, leading[:, None], 0.0) + jnp.where(
        second_hit, trailing[:, None], 0.0
    )


def combine(earlier, later):
    first_top, first_sum, first_acc = earlier
    second_top, second_sum, second_acc = later
    joint_top = jnp.maximum(first_top, second_top)
    first_factor = jnp.exp(first_top - joint_top)
    second_factor = jnp.exp(second_top - joint_top)
    return (
        joint_top,
        first_sum * first_factor + second_sum * second_factor,
        first_acc * first_factor[..., None] + second_acc * second_factor[..., None],
    )


def slot_plan(page_dest, pages_dev, slot_count, slots_dev, replicas, groups):
    part_index = page_dest // slot_count
    within = page_dest % slot_count
    target = within // slots_dev * replicas + part_index
    position = within % slots_dev
    per_device = target.reshape(-1, pages_dev)
    onehot = (per_device[:, :, None] == jnp.arange(groups, dtype=jnp.int32)[None, None, :]).astype(
        jnp.int32
    )
    before = jnp.cumsum(onehot, axis=1) - onehot
    ranking = jnp.sum(before * onehot, axis=2).reshape(-1)
    return (target, position, ranking)


def partial_attention(page_block, owners, page_pos, lengths, grouped, score_scale):
    head_dim = grouped.shape[-1]
    page_len = page_block.shape[2]
    requests = grouped.shape[1]
    clipped = jnp.minimum(owners, requests - 1)
    length_cap = jnp.take(lengths, clipped)
    offsets = page_pos[:, None] * page_len + jnp.arange(page_len, dtype=jnp.int32)[None, :]
    is_live = (owners < requests)[:, None] & (offsets < length_cap[:, None])
    live_mask = is_live[None, :, None, None, :]
    asked_rows = jnp.take(grouped, clipped, axis=1)
    scores = (
        jnp.einsum(
            "spkgd,pktd->spkgt",
            asked_rows,
            page_block[..., :head_dim],
            preferred_element_type=jnp.float32,
        )
        * score_scale
    )
    scores = jnp.where(live_mask, scores, NEG_FILL)
    members = owners[:, None] == jnp.arange(requests, dtype=jnp.int32)[None, :]
    page_top = jnp.max(scores, axis=4)
    row_top = jnp.max(
        jnp.where(members[None, :, :, None, None], page_top[:, :, None], NEG_FILL), axis=1
    )
    weights = jnp.where(
        live_mask, jnp.exp(scores - jnp.take(row_top, clipped, axis=1)[..., None]), 0.0
    )
    member_mask = members.astype(jnp.float32)
    totals = jnp.einsum("pr,spkg->srkg", member_mask, jnp.sum(weights, axis=4), precision=HIGHEST)
    page_out = jnp.einsum(
        "spkgt,pktd->spkgd",
        weights.astype(jnp.bfloat16),
        page_block[..., head_dim:],
        preferred_element_type=jnp.float32,
    )
    weighted = jnp.einsum("pr,spkgd->srkgd", member_mask, page_out, precision=HIGHEST)
    return (row_top, totals, weighted)


def body(
    lengths,
    page_owner,
    page_index,
    page_dest,
    src_cache,
    queries,
    new_kv,
    hidden_in,
    out_weight,
    norm_gain,
    router,
    routes,
    w_gate,
    w_up,
    w_down,
):
    seq_count = lax.axis_size(SEQ)
    head_count = lax.axis_size(HEAD)
    device_count = seq_count * head_count
    seq_pos = lax.axis_index(SEQ)
    head_pos = lax.axis_index(HEAD)
    pages_dev = src_cache.shape[0]
    page_total = page_dest.shape[0]
    replicas = head_count // KVH
    groups = seq_count * replicas
    slot_count = page_total // replicas
    slots_dev = pages_dev * KVH
    capacity = (slots_dev + device_count - 1) // device_count
    group_size = HQ // KVH
    step_count = queries.shape[0]
    row_count = step_count * REQS
    source = seq_pos * head_count + head_pos
    target, position, ranking = slot_plan(
        page_dest, pages_dev, slot_count, slots_dev, replicas, groups
    )
    local_target = lax.dynamic_slice_in_dim(target, source * pages_dev, pages_dev)
    local_rank = lax.dynamic_slice_in_dim(ranking, source * pages_dev, pages_dev)
    wanted = jnp.arange(groups * capacity, dtype=jnp.int32)
    matches = (local_target[None, :] == (wanted // capacity)[:, None]) & (
        local_rank[None, :] == (wanted % capacity)[:, None]
    )
    picked_page = jnp.sum(
        jnp.where(matches, jnp.arange(pages_dev, dtype=jnp.int32)[None, :], 0), axis=1
    )
    filled = jnp.any(matches, axis=1)
    packed = jnp.where(
        filled[:, None, None, None],
        jnp.take(src_cache, picked_page, axis=0),
        jnp.zeros((), jnp.bfloat16),
    )
    packed = packed.reshape(seq_count, replicas, capacity, KVH, PAGE, 2 * HD).transpose(
        0, 3, 1, 2, 4, 5
    )
    arrived = lax.all_to_all(
        packed.reshape(device_count, capacity, PAGE, 2 * HD),
        SEQ_HEAD,
        split_axis=0,
        concat_axis=0,
        tiled=True,
    )
    arrived = arrived.reshape(device_count * capacity, PAGE, 2 * HD)
    my_group = seq_pos * replicas + head_pos % replicas
    slot_ids = jnp.arange(slots_dev, dtype=jnp.int32)
    holders = (target[None, :] == my_group) & (position[None, :] == slot_ids[:, None])
    flat_index = jnp.arange(page_total, dtype=jnp.int32) // pages_dev * capacity + ranking
    chosen = jnp.sum(jnp.where(holders, flat_index[None, :], 0), axis=1)
    page_pool = jnp.take(arrived, chosen, axis=0)
    grouped = queries.reshape(step_count, REQS, KVH, group_size, HD)
    score_scale = HD ** (-0.5)
    kv_head = head_pos // replicas
    owners = jnp.sum(jnp.where(holders, page_owner[None, :], 0), axis=1)
    places = jnp.sum(jnp.where(holders, page_index[None, :], 0), axis=1)
    own_queries = lax.dynamic_slice_in_dim(grouped, kv_head, 1, axis=2)
    row_top, totals, weighted = partial_attention(
        page_pool[:, None], owners, places, lengths, own_queries, score_scale
    )
    owned_head = (jnp.arange(KVH, dtype=jnp.int32) == kv_head)[None, None, :, None]
    row_top = jnp.where(owned_head, row_top, NEG_FILL)
    totals = jnp.where(owned_head, totals, 0.0)
    weighted = jnp.where(owned_head[..., None], weighted, 0.0)
    row_top, totals, weighted = joined_all(
        (
            row_top.reshape(step_count, REQS, HQ),
            totals.reshape(step_count, REQS, HQ),
            weighted.reshape(step_count, REQS, HQ, HD),
        ),
        SEQ_HEAD,
        combine,
    )
    fresh_scores = (
        jnp.einsum(
            "srkgd,urkd->srkgu", grouped, new_kv[..., :HD], preferred_element_type=jnp.float32
        )
        * score_scale
    )
    causal = (jnp.arange(step_count)[:, None] >= jnp.arange(step_count)[None, :])[:, None, None, :]
    fresh_scores = jnp.where(
        causal, fresh_scores.reshape(step_count, REQS, HQ, step_count), NEG_FILL
    )
    joint_top = jnp.maximum(row_top, jnp.max(fresh_scores, axis=3))
    factor = jnp.exp(row_top - joint_top)
    fresh_weights = jnp.where(causal, jnp.exp(fresh_scores - joint_top[..., None]), 0.0)
    totals = totals * factor + jnp.sum(fresh_weights, axis=3)
    fresh_rounded = fresh_weights.reshape(step_count, REQS, KVH, group_size, step_count).astype(
        jnp.bfloat16
    )
    fresh_out = jnp.einsum(
        "srkgu,urkd->srkgd", fresh_rounded, new_kv[..., HD:], preferred_element_type=jnp.float32
    )
    weighted = weighted * factor[..., None] + fresh_out.reshape(step_count, REQS, HQ, HD)
    attended = (weighted / totals[..., None]).reshape(row_count, HQ * HD).astype(jnp.bfloat16)
    attn_out = jnp.dot(attended, out_weight, preferred_element_type=jnp.float32)
    middle = hidden_in.reshape(row_count, -1).astype(jnp.float32) + attn_out
    gain_row = norm_gain.astype(jnp.float32)[None, :]
    squares, routed = (
        over_axes(jnp.sum(middle * middle, axis=1), SEQ_HEAD),
        over_axes(
            jnp.dot(middle * gain_row, router.astype(jnp.float32), precision=HIGHEST), SEQ_HEAD
        ),
    )
    inverse_rms = lax.rsqrt(squares / D + EPSILON)
    logits = routed * inverse_rms[:, None]
    normed = (middle * inverse_rms[:, None] * gain_row).astype(jnp.bfloat16)
    features = lax.all_gather(normed, SEQ_HEAD, axis=1, tiled=True)
    mixture = gate_mix(logits, routes.reshape(row_count, TOPK))
    local_experts = w_gate.shape[0]
    local_mix = lax.dynamic_slice_in_dim(mixture, seq_pos * local_experts, local_experts, axis=1)
    gate_act = jnp.einsum("rd,edf->erf", features, w_gate, preferred_element_type=jnp.float32)
    upward = jnp.einsum("rd,edf->erf", features, w_up, preferred_element_type=jnp.float32)
    inner_act = (jax.nn.silu(gate_act) * upward).astype(jnp.bfloat16)
    produced = jnp.einsum("erf,efd->erd", inner_act, w_down, preferred_element_type=jnp.float32)
    moe_out = sum_all_axes_2(jnp.sum(local_mix.T[:, :, None] * produced, axis=0).T, SEQ_HEAD, 0)
    mixed = (middle + moe_out.T).astype(jnp.bfloat16).reshape(step_count, REQS, -1)
    return (page_pool[None], mixed)


def solution(mesh):
    split = Mesh(mesh.devices.reshape(4, 2, 4, 4), ("seq_0", "seq_1", "head_0", "head_1"))
    in_specs = (
        P(),
        P(),
        P(),
        P(),
        P(SEQ_HEAD, None, None, None),
        P(),
        P(),
        P(None, None, SEQ_HEAD),
        P(None, SEQ_HEAD),
        P(SEQ_HEAD),
        P(SEQ_HEAD, None),
        P(),
        P(SEQ, None, HEAD),
        P(SEQ, None, HEAD),
        P(SEQ, HEAD, None),
    )
    out_specs = (P(HEAD, SEQ, None, None), P(None, None, SEQ_HEAD))
    return jax.shard_map(body, mesh=split, in_specs=in_specs, out_specs=out_specs, check_vma=False)
```

profile of v0, /device:TPU:1, one launch (start us, length us, event | category | flops | bytes accessed | tf_op | source)
XLA Modules:
  0.0 604.6 jit_solution(12945465828086669318)
XLA Ops:
  9.1 2.7 gather_fusion
  11.9 2.7 select_bitcast_fusion
  14.6 2.3 copy.230
  16.9 12.0 %all-to-all-start = ((bf16[128,1,64,256]{3,2,1,0:T(8,128)(2,1)}), bf16[128,1,64,256]{3,2,1,0:T(8,128)(2,1)}, u32[]{:S(2)}, u32[]{:S(2)}) async-start(bf16[128,1,64,256]{3,2,1,0:T(8,128)(2,1)} %bitcast.483), calls=%async_computation | async-start | bytes 8388608 | tf_op jit(solution)/shard_map/all_to_all | solution.py:207
  32.0 9.8 %fusion.130 = (s32[96]{0:T(128)S(1)}, s32[96]{0:T(128)S(1)}) fusion(s32[]{:T(128)} %bitcast.17, s32[]{:T(128)} %bitcast.18, s32[]{:T(128)} %bitcast.19, s32[]{:T(128)} %bitcast.20, s32[]{:T(128)} %bitcast.21, s32[]{:T(128)} %bitcast.22, s32[]{:T(128)} %bitcast.23, s32[]{:T(128)} %bitcast.24, s32[]{:T(128)} %bitcast.25, s32[]{:T(128)} %bitcast.26, ...), kind=kLoop, calls=%fused_computation.273 | loop fusion | flops 4032 | bytes 1600 | tf_op jit(solution)/shard_map/jit(_take)/select_n | solution.py:118
  41.9 39.2 %all-to-all-done = bf16[128,1,64,256]{3,2,1,0:T(8,128)(2,1)} async-done(((bf16[128,1,64,256]{3,2,1,0:T(8,128)(2,1)}), bf16[128,1,64,256]{3,2,1,0:T(8,128)(2,1)}, u32[]{:S(2)}, u32[]{:S(2)}) %all-to-all-start) | async-done | bytes 4194336 | tf_op jit(solution)/shard_map/all_to_all | solution.py:207
  81.2 3.0 gather_fusion.1
  94.3 9.0 %all_gather.49 = f32[4,2,16,32]{3,2,1,0:T(8,128)S(1)} all-gather(f32[1,2,16,32]{3,2,1,0:T(8,128)S(1)} %copy.236), channel_id=1, replica_groups=mesh['seq_0'=4,'seq_1'=2,'head_0'=4,'head_1'=4] {'seq_0'}, dimensions={0}, use_global_device_ids=true | all-gather | bytes 20480 | tf_op jit(solution)/shard_map/all_gather | solution.py:26
  103.3 17.1 %all-gather.5.cloned.1.call-done = f32[4,2,16,32,128]{4,3,2,1,0:T(8,128)} async-done(((f32[1,2,16,32,128]{4,3,2,1,0:T(8,128)}), f32[4,2,16,32,128]{4,3,2,1,0:T(8,128)}) %all-gather.5.cloned.1.call-update) | async-done | bytes 2097168 | tf_op jit(solution)/shard_map/all_gather | solution.py:26
  120.4 2.9 fusion.45
  123.4 9.1 %all_gather.56 = f32[4,2,16,32]{3,2,1,0:T(8,128)S(1)} all-gather(f32[1,2,16,32]{3,2,1,0:T(8,128)S(1)} %copy.255), channel_id=1, replica_groups=mesh['seq_0'=4,'seq_1'=2,'head_0'=4,'head_1'=4] {'seq_0'}, dimensions={0}, use_global_device_ids=true | all-gather | bytes 20480 | tf_op jit(solution)/shard_map/all_gather | solution.py:26
  132.6 5.1 all_gather.51
  137.8 2.3 fusion.44
  142.0 9.2 %all_gather.53 = f32[4,2,16,32]{3,2,1,0:T(8,128)S(1)} all-gather(f32[1,2,16,32]{3,2,1,0:T(8,128)S(1)} %get-tuple-element.32), channel_id=1, replica_groups=mesh['seq_0'=4,'seq_1'=2,'head_0'=4,'head_1'=4] {'head_0'}, dimensions={0}, use_global_device_ids=true | all-gather | bytes 20480 | tf_op jit(solution)/shard_map/all_gather | solution.py:26
  151.3 18.7 %all-gather.9.cloned.1.call-done = f32[4,2,16,32,128]{4,3,2,1,0:T(8,128)} async-done(((f32[1,2,16,32,128]{4,3,2,1,0:T(8,128)}), f32[4,2,16,32,128]{4,3,2,1,0:T(8,128)}) %all-gather.9.cloned.1.call-update) | async-done | bytes 2097168 | tf_op jit(solution)/shard_map/all_gather | solution.py:26
  170.0 2.9 fusion.39
  173.1 2.4 fusion.152
  175.8 9.0 %all_gather.58 = f32[4,2,16,32]{3,2,1,0:T(8,128)S(1)} all-gather(f32[1,2,16,32]{3,2,1,0:T(8,128)S(1)} %get-tuple-element.31), channel_id=1, replica_groups=mesh['seq_0'=4,'seq_1'=2,'head_0'=4,'head_1'=4] {'head_0'}, dimensions={0}, use_global_device_ids=true | all-gather | bytes 20480 | tf_op jit(solution)/shard_map/all_gather | solution.py:26
  184.8 11.2 %all_gather.55 = f32[4,2,16,32]{3,2,1,0:T(8,128)S(1)} all-gather(f32[1,2,16,32]{3,2,1,0:T(8,128)S(1)} %get-tuple-element.30), channel_id=1, replica_groups=mesh['seq_0'=4,'seq_1'=2,'head_0'=4,'head_1'=4] {'head_1'}, dimensions={0}, use_global_device_ids=true | all-gather | bytes 20480 | tf_op jit(solution)/shard_map/all_gather | solution.py:26
  197.3 9.7 %all_gather.59 = f32[4,2,16,32]{3,2,1,0:T(8,128)S(1)} all-gather(f32[1,2,16,32]{3,2,1,0:T(8,128)S(1)} %get-tuple-element.29), channel_id=1, replica_groups=mesh['seq_0'=4,'seq_1'=2,'head_0'=4,'head_1'=4] {'head_1'}, dimensions={0}, use_global_device_ids=true | all-gather | bytes 20480 | tf_op jit(solution)/shard_map/all_gather | solution.py:26
  212.1 3.6 multiply_reduce_fusion
  215.9 8.8 %all-reduce.6 = (f32[32]{0:T(128)S(1)}, f32[32,8]{0,1:T(8,128)S(1)}) all-reduce(f32[32]{0:T(128)S(1)} %get-tuple-element.95, f32[32,8]{0,1:T(8,128)S(1)} %fusion.112), channel_id=1, replica_groups=mesh['seq_0'=4,'seq_1'=2,'head_0'=4,'head_1'=4] {'seq_0'}, use_global_device_ids=true, to_apply=%region_17.18 | all-reduce | flops 288 | bytes 2304 | tf_op jit(solution)/shard_map/psum | solution.py:35
  224.8 11.8 %all-reduce.7 = (f32[32]{0:T(128)S(1)}, f32[32,8]{0,1:T(8,128)S(1)}) all-reduce(f32[32]{0:T(128)S(1)} %get-tuple-element.13, f32[32,8]{0,1:T(8,128)S(1)} %get-tuple-element.14), channel_id=1, replica_groups=mesh['seq_0'=4,'seq_1'=2,'head_0'=4,'head_1'=4] {'seq_1'}, use_global_device_ids=true, to_apply=%region_18.19 | all-reduce | flops 288 | bytes 2304 | tf_op jit(solution)/shard_map/psum | solution.py:35
  236.6 6.7 %all-reduce.5 = (f32[32]{0:T(128)S(1)}, f32[32,8]{0,1:T(8,128)S(1)}) all-reduce(f32[32]{0:T(128)S(1)} %get-tuple-element.15, f32[32,8]{0,1:T(8,128)S(1)} %get-tuple-element.16), channel_id=1, replica_groups=mesh['seq_0'=4,'seq_1'=2,'head_0'=4,'head_1'=4] {'head_0'}, use_global_device_ids=true, to_apply=%region_19.20 | all-reduce | flops 288 | bytes 2304 | tf_op jit(solution)/shard_map/psum | solution.py:35
  243.3 8.3 %all-reduce.4 = (f32[32]{0:T(128)S(1)}, f32[32,8]{0,1:T(8,128)S(1)}) all-reduce(f32[32]{0:T(128)S(1)} %get-tuple-element.11, f32[32,8]{0,1:T(8,128)S(1)} %get-tuple-element.12), channel_id=1, replica_groups=mesh['seq_0'=4,'seq_1'=2,'head_0'=4,'head_1'=4] {'head_1'}, use_global_device_ids=true, to_apply=%region_20.21 | all-reduce | flops 288 | bytes 2304 | tf_op jit(solution)/shard_map/psum | solution.py:35
  251.6 62.4 %all_gather.60 = bf16[32,4096]{0,1:T(8,128)(2,1)S(1)} all-gather(bf16[32,32]{0,1:T(8,128)(2,1)S(1)} %multiply_convert_fusion), channel_id=1, replica_groups=mesh['seq_0'=4,'seq_1'=2,'head_0'=4,'head_1'=4] {'seq_0','seq_1','head_0..., dimensions={1}, use_global_device_ids=true | all-gather | bytes 264192 | tf_op jit(solution)/shard_map/all_gather | solution.py:277
  314.1 3.0 fusion.14
  317.1 5.1 fusion
  322.9 4.9 fusion.144
  327.8 2.9 copy.267
  330.8 3.1 copy.266
  334.7 14.0 %reduce-scatter.31.cloned.1.call-done = f32[32,8,32]{2,1,0:T(8,128)} async-done(((f32[128,8,32]{2,1,0:T(8,128)}), f32[32,8,32]{2,1,0:T(8,128)}) %reduce-scatter.31.cloned.1.call-update) | async-done | bytes 32784 | tf_op jit(solution)/shard_map/reduce_scatter | solution.py:56
  348.8 23.5 %reduce-scatter.25.cloned.1.call-done = f32[32,8,32]{2,1,0:T(8,128)} async-done(((f32[128,8,32]{2,1,0:T(8,128)}), f32[32,8,32]{2,1,0:T(8,128)}) %reduce-scatter.25.cloned.1.call-update) | async-done | bytes 32784 | tf_op jit(solution)/shard_map/reduce_scatter | solution.py:56
  372.4 34.3 %reduce-scatter.13.cloned.1.call-done = f32[32,8,32]{1,0,2:T(8,128)} async-done(((f32[128,8,32]{1,0,2:T(8,128)}), f32[32,8,32]{1,0,2:T(8,128)}) %reduce-scatter.13.cloned.1.call-update) | async-done | bytes 32784 | tf_op jit(solution)/shard_map/reduce_scatter | solution.py:56
  408.8 18.5 %reduce-scatter.33.cloned.1.call-done = f32[8,8,32]{2,1,0:T(8,128)} async-done(((f32[32,8,32]{2,1,0:T(8,128)}), f32[8,8,32]{2,1,0:T(8,128)}) %reduce-scatter.33.cloned.1.call-update) | async-done | bytes 8208 | tf_op jit(solution)/shard_map/reduce_scatter | solution.py:56
  427.4 22.6 %reduce-scatter.27.cloned.1.call-done = f32[8,8,32]{2,1,0:T(8,128)} async-done(((f32[32,8,32]{2,1,0:T(8,128)}), f32[8,8,32]{2,1,0:T(8,128)}) %reduce-scatter.27.cloned.1.call-update) | async-done | bytes 8208 | tf_op jit(solution)/shard_map/reduce_scatter | solution.py:56
  452.6 12.7 %reduce-scatter.15.cloned.1.call-done = f32[16,8,32]{1,0,2:T(8,128)} async-done(((f32[32,8,32]{1,0,2:T(8,128)}), f32[16,8,32]{1,0,2:T(8,128)}) %reduce-scatter.15.cloned.1.call-update) | async-done | bytes 16400 | tf_op jit(solution)/shard_map/reduce_scatter | solution.py:56
  467.1 4.1 bitcast_select_fusion.1
  471.1 8.5 %reduce-scatter.19.cloned.1.call-done = f32[64,8,32]{2,1,0:T(8,128)} async-done(((f32[128,8,32]{2,1,0:T(8,128)}), f32[64,8,32]{2,1,0:T(8,128)}) %reduce-scatter.19.cloned.1.call-update) | async-done | bytes 65552 | tf_op jit(solution)/shard_map/reduce_scatter | solution.py:56
  479.6 13.6 %reduce-scatter.35.cloned.1.call-done = f32[4,8,32]{2,1,0:T(8,128)} async-done(((f32[8,8,32]{2,1,0:T(8,128)}), f32[4,8,32]{2,1,0:T(8,128)}) %reduce-scatter.35.cloned.1.call-update) | async-done | bytes 4112 | tf_op jit(solution)/shard_map/reduce_scatter | solution.py:56
  493.3 13.8 %all-reduce.3 = f32[4,8,32]{2,1,0:T(8,128)S(1)} all-reduce(f32[4,8,32]{2,1,0:T(8,128)} %reduce-scatter.35.cloned.1.call-done), channel_id=17, replica_groups=mesh['seq_0'=4,'seq_1'=2,'head_0'=4,'head_1'=4] {'head_0'}, use_global_device_ids=true, to_apply=%region_38.39.clone | all-reduce | flops 1024 | bytes 8192
  507.7 7.4 %reduce-scatter.29.cloned.1.call-done = f32[2,8,32]{2,1,0:T(8,128)} async-done(((f32[8,8,32]{2,1,0:T(8,128)}), f32[2,8,32]{2,1,0:T(8,128)}) %reduce-scatter.29.cloned.1.call-update) | async-done | bytes 2064 | tf_op jit(solution)/shard_map/reduce_scatter | solution.py:56
  515.1 5.0 all-reduce.2
  520.8 16.5 %reduce-scatter.17.cloned.1.call-done = f32[4,8,32]{2,1,0:T(8,128)} async-done(((f32[16,8,32]{2,1,0:T(8,128)}), f32[4,8,32]{2,1,0:T(8,128)}) %reduce-scatter.17.cloned.1.call-update) | async-done | bytes 4112 | tf_op jit(solution)/shard_map/reduce_scatter | solution.py:56
  537.3 13.7 %all-reduce = f32[4,8,32]{2,1,0:T(8,128)S(1)} all-reduce(f32[4,8,32]{2,1,0:T(8,128)} %reduce-scatter.17.cloned.1.call-done), channel_id=5, replica_groups=mesh['seq_0'=4,'seq_1'=2,'head_0'=4,'head_1'=4] {'head_1'}, use_global_device_ids=true, to_apply=%region_26.27.clone | all-reduce | flops 1024 | bytes 8192
  551.0 9.2 %reduce-scatter.21.cloned.1.call-done = f32[16,8,32]{2,1,0:T(8,128)} async-done(((f32[64,8,32]{2,1,0:T(8,128)}), f32[16,8,32]{2,1,0:T(8,128)}) %reduce-scatter.21.cloned.1.call-update) | async-done | bytes 16400 | tf_op jit(solution)/shard_map/reduce_scatter | solution.py:56
  560.8 21.8 %reduce-scatter.23.cloned.1.call-done = f32[4,8,32]{2,1,0:T(8,128)} async-done(((f32[16,8,32]{2,1,0:T(8,128)}), f32[4,8,32]{2,1,0:T(8,128)}) %reduce-scatter.23.cloned.1.call-update) | async-done | bytes 4112 | tf_op jit(solution)/shard_map/reduce_scatter | solution.py:56
  582.7 14.0 %all-reduce.1 = f32[4,8,32]{2,1,0:T(8,128)S(1)} all-reduce(f32[4,8,32]{2,1,0:T(8,128)} %reduce-scatter.23.cloned.1.call-done), channel_id=9, replica_groups=mesh['seq_0'=4,'seq_1'=2,'head_0'=4,'head_1'=4] {'seq_0'}, use_global_device_ids=true, to_apply=%region_30.31.clone | all-reduce | flops 1024 | bytes 8192
  (201 shorter events, 36.0 us)
Async XLA Ops:
  7.2 2.0 copy-start
  16.9 12.0 %copy-start.6 = (bf16[2,16,4096]{2,1,0:T(8,128)(2,1)S(1)}, bf16[2,16,4096]{2,1,0:T(8,128)(2,1)}, u32[]{:S(2)}) copy-start(bf16[2,16,4096]{2,1,0:T(8,128)(2,1)} %param.20) | copy-start | bytes 786436
  16.9 12.4 %copy-start.10 = (s32[1536]{0:T(1024)S(1)}, s32[1536]{0:T(1024)}, u32[]{:S(2)}) copy-start(s32[1536]{0:T(1024)} %param.18) | copy-start | bytes 18436
  16.9 12.5 %copy-start.12 = (s32[1536]{0:T(1024)S(1)}, s32[1536]{0:T(1024)}, u32[]{:S(2)}) copy-start(s32[1536]{0:T(1024)} %param.17) | copy-start | bytes 18436
  16.9 12.5 %copy-start.13 = (s32[1536]{0:T(1024)S(1)}, s32[1536]{0:T(1024)}, u32[]{:S(2)}) copy-start(s32[1536]{0:T(1024)} %param.16) | copy-start | bytes 18436
  16.9 14.4 %copy-start.9 = (s32[16]{0:T(128)S(1)}, s32[16]{0:T(128)}, u32[]{:S(2)}) copy-start(s32[16]{0:T(128)} %param.15) | copy-start | bytes 196
  16.9 64.3 %all-to-all-start = ((bf16[128,1,64,256]{3,2,1,0:T(8,128)(2,1)}), bf16[128,1,64,256]{3,2,1,0:T(8,128)(2,1)}, u32[]{:S(2)}, u32[]{:S(2)}) async-start(bf16[128,1,64,256]{3,2,1,0:T(8,128)(2,1)} %bitcast.483), calls=%async_computation | async-start | bytes 8388608 | tf_op jit(solution)/shard_map/all_to_all | solution.py:207
  28.9 91.6 %all-gather.5.cloned.1.call-start = ((), (), s32[]{:S(2)}) async-start(), calls=%async_computation.13 | async-start | bytes 2621440 | tf_op jit(solution)/shard_map/all_gather | solution.py:26
  84.2 1.7 copy-start.2
  84.2 3.3 copy-start.7
  85.8 1.7 copy-start.4
  93.2 44.5 %all-gather.7.cloned.1.call-start = ((), (), s32[]{:S(2)}) async-start(), calls=%async_computation.14 | async-start | bytes 1572864 | tf_op jit(solution)/shard_map/all_gather | solution.py:26
  123.3 49.6 %copy-start.11 = (bf16[2,16,32]{2,1,0:T(8,128)(2,1)S(1)}, bf16[2,16,32]{2,1,0:T(8,128)(2,1)}, u32[]{:S(2)}) copy-start(bf16[2,16,32]{2,1,0:T(8,128)(2,1)} %param.22) | copy-start | bytes 6148
  123.3 46.7 %all-gather.9.cloned.1.call-start = ((), (), s32[]{:S(2)}) async-start(), calls=%async_computation.15 | async-start | bytes 2621440 | tf_op jit(solution)/shard_map/all_gather | solution.py:26
  123.4 49.6 %copy-start.8 = (bf16[2,16,8,256]{3,2,1,0:T(8,128)(2,1)S(1)}, bf16[2,16,8,256]{3,2,1,0:T(8,128)(2,1)}, u32[]{:S(2)}) copy-start(bf16[2,16,8,256]{3,2,1,0:T(8,128)(2,1)} %param.21) | copy-start | bytes 393220
  140.1 35.6 %copy-start.16 = (bf16[32]{0:T(256)(128)(2,1)S(1)}, bf16[32]{0:T(256)(128)(2,1)}, u32[]{:S(2)}) copy-start(bf16[32]{0:T(256)(128)(2,1)} %param.24) | copy-start | bytes 196
  140.1 35.6 %copy-start.14 = (s32[2,16,2]{1,2,0:T(2,128)S(1)}, s32[2,16,2]{1,2,0:T(2,128)}, u32[]{:S(2)}) copy-start(s32[2,16,2]{1,2,0:T(2,128)} %param.26) | copy-start | bytes 772
  140.1 68.6 %all-gather.11.cloned.1.call-start = ((), (), s32[]{:S(2)}) async-start(), calls=%async_computation.16 | async-start | bytes 2621440 | tf_op jit(solution)/shard_map/all_gather | solution.py:26
  172.9 175.9 %reduce-scatter.31.cloned.1.call-start = ((), (), s32[]{:S(2)}) async-start(), calls=%async_computation.26 | async-start | bytes 655360 | tf_op jit(solution)/shard_map/reduce_scatter | solution.py:56
  210.5 1.6 copy-start.5
  212.1 3.6 copy-start.15
  330.7 76.1 %copy-start.3 = (f32[128,8,32]{1,0,2:T(8,128)S(1)}, f32[128,8,32]{1,0,2:T(8,128)}, u32[]{:S(2)}) copy-start(f32[128,8,32]{1,0,2:T(8,128)} %get-tuple-element.40) | copy-start | bytes 393220
  330.8 41.6 %reduce-scatter.25.cloned.1.call-start = ((), (), s32[]{:S(2)}) async-start(), calls=%async_computation.23 | async-start | bytes 655360 | tf_op jit(solution)/shard_map/reduce_scatter | solution.py:56
  333.9 116.2 %copy-start.20 = (u32[128]{0:T(128)S(1)}, u32[128]{0:T(128)}, u32[]{:S(2)}) copy-start(u32[128]{0:T(128)} %constant.244) | copy-start | bytes 1540
  333.9 116.8 %copy-start.19 = (u32[128]{0:T(128)S(1)}, u32[128]{0:T(128)}, u32[]{:S(2)}) copy-start(u32[128]{0:T(128)} %constant.240) | copy-start | bytes 1540
  333.9 117.4 %copy-start.18 = (u32[128]{0:T(128)S(1)}, u32[128]{0:T(128)}, u32[]{:S(2)}) copy-start(u32[128]{0:T(128)} %constant.236) | copy-start | bytes 1540
  333.9 118.0 %copy-start.17 = (u32[128]{0:T(128)S(1)}, u32[128]{0:T(128)}, u32[]{:S(2)}) copy-start(u32[128]{0:T(128)} %constant.232) | copy-start | bytes 1540
  333.9 72.8 %reduce-scatter.13.cloned.1.call-start = ((), (), s32[]{:S(2)}) async-start(), calls=%async_computation.17 | async-start | bytes 2621440 | tf_op jit(solution)/shard_map/reduce_scatter | solution.py:56
  334.7 92.6 %reduce-scatter.33.cloned.1.call-start = ((), (), s32[]{:S(2)}) async-start(), calls=%async_computation.27 | async-start | bytes 163840 | tf_op jit(solution)/shard_map/reduce_scatter | solution.py:56
  348.8 101.2 %reduce-scatter.27.cloned.1.call-start = ((), (), s32[]{:S(2)}) async-start(), calls=%async_computation.24 | async-start | bytes 163840 | tf_op jit(solution)/shard_map/reduce_scatter | solution.py:56
  372.3 92.9 %reduce-scatter.15.cloned.1.call-start = ((), (), s32[]{:S(2)}) async-start(), calls=%async_computation.18 | async-start | bytes 786432 | tf_op jit(solution)/shard_map/reduce_scatter | solution.py:56
  406.8 72.8 %reduce-scatter.19.cloned.1.call-start = ((), (), s32[]{:S(2)}) async-start(), calls=%async_computation.20 | async-start | bytes 786432 | tf_op jit(solution)/shard_map/reduce_scatter | solution.py:56
  408.8 84.5 %reduce-scatter.35.cloned.1.call-start = ((), (), s32[]{:S(2)}) async-start(), calls=%async_computation.28 | async-start | bytes 49152 | tf_op jit(solution)/shard_map/reduce_scatter | solution.py:56
  427.4 87.8 %reduce-scatter.29.cloned.1.call-start = ((), (), s32[]{:S(2)}) async-start(), calls=%async_computation.25 | async-start | bytes 40960 | tf_op jit(solution)/shard_map/reduce_scatter | solution.py:56
  450.0 87.3 %reduce-scatter.17.cloned.1.call-start = ((), (), s32[]{:S(2)}) async-start(), calls=%async_computation.19 | async-start | bytes 81920 | tf_op jit(solution)/shard_map/reduce_scatter | solution.py:56
  467.0 131.0 %copy-start.1 = (bf16[12,8,64,256]{3,2,1,0:T(8,128)(2,1)S(1)}, bf16[12,8,64,256]{3,2,1,0:T(8,128)(2,1)}, u32[]{:S(2)}) copy-start(bf16[12,8,64,256]{3,2,1,0:T(8,128)(2,1)} %param.19) | copy-start | bytes 9437188
  467.0 93.2 %reduce-scatter.21.cloned.1.call-start = ((), (), s32[]{:S(2)}) async-start(), calls=%async_computation.21 | async-start | bytes 327680 | tf_op jit(solution)/shard_map/reduce_scatter | solution.py:56
  479.6 103.1 %reduce-scatter.23.cloned.1.call-start = ((), (), s32[]{:S(2)}) async-start(), calls=%async_computation.22 | async-start | bytes 81920 | tf_op jit(solution)/shard_map/reduce_scatter | solution.py:56
Sparse Core Ops, SparseCore 0:
  93.4 27.0 all-gather.4
  123.4 11.9 all-gather.6
  140.2 29.7 all-gather.8
  173.0 31.3 all-gather.10
  330.9 17.8 reduce-scatter.30
  351.0 21.2 reduce-scatter.24
  374.7 31.9 reduce-scatter.12
  409.1 18.2 reduce-scatter.32
  429.7 20.2 reduce-scatter.26
  452.2 13.0 reduce-scatter.14
  467.6 11.9 reduce-scatter.18
  481.7 11.4 reduce-scatter.34
  495.6 19.4 reduce-scatter.28
  517.3 19.9 reduce-scatter.16
  539.5 20.6 reduce-scatter.20
  562.4 20.2 reduce-scatter.22
where the time goes:
time: 611 us; the launch traced here: 605 us
  waiting for transfers between devices  279 us (46%)
  blocking collectives  208 us (34%)
  local copies, waits for them, and re-layouts  42 us (7%)
  other arithmetic  29.7 us (5%)
  matrix products  18.5 us (3%)
  between operations  14.7 us (2%)
  starting transfers between devices  12.6 us (2%)
    reduce_scatter x12, waiting for transfers between devices, own_block(): blocks = lax.psum_scatter(blocks, axes[k], scatter_dimension=0, tiled=True)  203 us
    all_gather x8, blocking collectives, joined_all(): pieces = jax.tree.map(lambda part: lax.all_gather(part, axis), array)  64 us
    all_gather x1, blocking collectives, body(): features = lax.all_gather(normed, SEQ_HEAD, axis=1, tiled=True)  62.4 us
    unnamed x4, blocking collectives  46.5 us
    all_to_all x1, waiting for transfers between devices, body(): lax.all_to_all(packed.reshape(device_count, capacity, PAGE, 2 * HD), SEQ_...  39.2 us
    all_gather x4, waiting for transfers between devices, joined_all(): pieces = jax.tree.map(lambda part: lax.all_gather(part, axis), array)  35.8 us
    psum x4, blocking collectives, over_axes(): array = lax.psum(array, axis)  35.6 us
  transfers between devices with their start and end apart: 17, of which 15 were waited for; matrix products, arithmetic and copies ran while one was open for 6% of the time, Pallas kernels for 0%

commit v1 on v0

v1 whole, which is shorter than its diff:
```python
import functools

import jax
import jax.numpy as jnp
from jax import lax
from jax.experimental import pallas as pl
from jax.experimental.pallas import tpu as pltpu
from jax.sharding import PartitionSpec as P

D = 4096
HQ = 32
KVH = 8
GROUP = HQ // KVH
HD = 128
EXPERTS = 8
PAGE = 64
REQS = 16
ROWS = 32
FF_DEV = 512
PG_DEV = 12
SLOTS = 768
SLOTS_DEV = 96
N_SEQ = 8
N_HEAD = 16
N_DEV = N_SEQ * N_HEAD
NEG_FILL = -1e30
EPSILON = 1e-05
HIGHEST = lax.Precision.HIGHEST
SCALE = HD ** (-0.5)
SEQ_HEAD = ("seq", "head")
BF16 = jnp.bfloat16
F32 = jnp.float32
BULK_STARTS = (0, 40, 20, 20, 20, 27)


def iota(shape, dim):
    return lax.broadcasted_iota(jnp.int32, shape, dim)


def dot(a, b, precision=None):
    return jnp.dot(a, b, preferred_element_type=F32, precision=precision)


def decode_kernel(
    lengths,
    page_owner,
    page_index,
    page_dest,
    src_hbm,
    queries_hbm,
    own_query,
    own_fresh,
    hidden,
    wo_hbm,
    gain,
    router,
    routes,
    wg_hbm,
    wu_hbm,
    wd_hbm,
    arrived,
    mixed,
    src,
    packed,
    queries,
    wo,
    wg,
    wu,
    wd,
    rs1_send,
    rs1_recv,
    ag1_send,
    ag1_recv,
    attended,
    ag2_send,
    ag2_recv,
    features,
    rs2_send,
    rs2_recv,
    src_sem,
    query_sem,
    weight_sem,
    own_sem,
    send_sem,
    recv_sem,
):
    seq = lax.axis_index("seq")
    head = lax.axis_index("head")
    me = seq * N_HEAD + head
    seqs = [lax.rem(seq + t, N_SEQ) for t in range(N_SEQ)]
    heads = [lax.rem(head + u, N_HEAD) for u in range(N_HEAD)]
    z, core, x, y = seq // 2, lax.rem(seq, 2), head // 4, lax.rem(head, 4)
    zs = [lax.rem(z + t, 4) for t in range(4)]
    cores = [lax.rem(core + t, 2) for t in range(2)]
    xs = [lax.rem(x + t, 4) for t in range(4)]
    ys = [lax.rem(y + t, 4) for t in range(4)]

    def page_copy(t):
        return pltpu.make_async_copy(src_hbm.at[:, seqs[t]], src.at[:, seqs[t]], src_sem.at[t])

    query_copy = pltpu.make_async_copy(queries_hbm, queries, query_sem)
    query_copy.start()
    for t in range(N_SEQ):
        page_copy(t).start()
    weight_copies = [
        pltpu.make_async_copy(a, b, weight_sem.at[n])
        for n, (a, b) in enumerate(((wo_hbm, wo), (wg_hbm, wg), (wu_hbm, wu), (wd_hbm, wd)))
    ]
    for copy in weight_copies:
        copy.start()

    barrier = pltpu.get_barrier_semaphore()

    def each_peer(act):
        for u in range(1, N_HEAD):
            act(seq, heads[u])

        def step(t, carry):
            to_seq = lax.rem(seq + t, N_SEQ)
            for u in range(N_HEAD):
                act(to_seq, heads[u])
            return carry

        lax.fori_loop(1, N_SEQ, step, 0)

    def greet(to_seq, to_head):
        pl.semaphore_signal(
            barrier,
            inc=1,
            device_id=(to_seq, to_head),
            device_id_type=pl.DeviceIdType.MESH,
        )

    each_peer(greet)

    def remote(source, target, phase, to_seq, to_head):
        return pltpu.make_async_remote_copy(
            src_ref=source,
            dst_ref=target,
            send_sem=send_sem.at[phase],
            recv_sem=recv_sem.at[phase],
            device_id=(to_seq, to_head),
            device_id_type=pl.DeviceIdType.MESH,
        )

    def all_but_one(buffer, phase):
        rest = buffer.at[pl.ds(0, N_DEV - 1)]
        return remote(rest, rest, phase, seq, head)

    lane = iota((1, PG_DEV * PAGE), 1)
    token_owner = jnp.full((1, PG_DEV * PAGE), REQS, jnp.int32)
    for p in range(PG_DEV):
        owner = page_owner[me * PG_DEV + p]
        limit = lengths[jnp.minimum(owner, REQS - 1)] - page_index[me * PG_DEV + p] * PAGE
        inside = (lane >= p * PAGE) & (lane < p * PAGE + jnp.minimum(limit, PAGE))
        token_owner = jnp.where(inside, owner, token_owner)

    def pack_pages():
        groups = []
        for p in range(PG_DEV):
            dest = page_dest[me * PG_DEV + p]
            upper = jnp.where(dest >= SLOTS, 1, 0)
            within = dest - upper * SLOTS
            target = jnp.int32(0)
            for n in range(1, N_SEQ):
                target = target + jnp.where(within >= n * SLOTS_DEV, 2, 0)
            groups.append(target + upper)

        def one(group, carry):
            page = jnp.int32(0)
            for p in range(PG_DEV):
                page = jnp.where(groups[p] == group, p, page)
            for k in range(KVH):
                packed[group, k] = src[page, k]
            return carry

        lax.fori_loop(0, 2 * N_SEQ, one, 0)

    started = [1]

    def start_bulk(count):
        for i in range(started[0], started[0] + count):
            j = (i * 37) % N_DEV
            to_seq = zs[j // 32] * 2 + cores[(j // 16) % 2]
            to_head = xs[(j // 4) % 4] * 4 + ys[j % 4]
            group = to_seq * 2 + lax.rem(to_head, 2)
            remote(packed.at[group, to_head // 2], arrived.at[me], 4, to_seq, to_head).start()
        started[0] += count

    query_copy.wait()
    row_request = lax.rem(iota((4 * ROWS, 1), 0), REQS)
    live = token_owner == row_request
    lane128 = iota((4 * ROWS, HD), 1)

    def attend_head(t):
        k = seqs[t]
        page_copy(t).wait()
        asked = jnp.concatenate(
            [
                queries[:, pl.ds(pl.multiple_of((k * GROUP + g) * HD, HD), HD)]
                for g in range(GROUP)
            ],
            axis=0,
        )
        keys = src[:, k, :, :HD].reshape(PG_DEV * PAGE, HD)
        values = src[:, k, :, HD:].reshape(PG_DEV * PAGE, HD)
        scores = (
            lax.dot_general(asked, keys, (((1,), (1,)), ((), ())), preferred_element_type=F32)
            * SCALE
        )
        scores = jnp.where(live, scores, NEG_FILL)
        top = jnp.max(scores, axis=1, keepdims=True)
        shift = jnp.where(top > -1e29, jnp.ceil(top * 0.25) * 4.0, NEG_FILL)
        weights = jnp.where(live, jnp.exp(scores - shift), 0.0)
        total = jnp.sum(weights, axis=1, keepdims=True)
        weighted = dot(weights.astype(BF16), values)
        total_high = total.astype(BF16).astype(F32)
        stats = jnp.where(
            lane128 < 32, shift, jnp.where(lane128 < 64, total_high, total - total_high)
        )
        parts = jnp.concatenate(
            [weighted.reshape(16, 8, HD), stats.reshape(16, 8, HD)], axis=1
        ).astype(BF16)
        rs1_send[pl.ds(k * N_HEAD, N_HEAD)] = parts

    def send_parts(t):
        for u in range(N_HEAD):
            if t or u:
                slot = seqs[t] * N_HEAD + heads[u]
                remote(rs1_send.at[slot], rs1_recv.at[me], 0, seqs[t], heads[u]).start()

    attend_head(0)
    rs1_recv[me] = rs1_send[me]
    attend_head(1)
    pl.semaphore_wait(barrier, N_DEV - 1)
    send_parts(0)
    send_parts(1)
    for t in range(2, N_SEQ):
        attend_head(t)
        send_parts(t)
    pack_pages()
    own_slot = pltpu.make_async_copy(
        packed.at[seq * 2 + lax.rem(head, 2), head // 2], arrived.at[me], own_sem
    )
    own_slot.start()
    start_bulk(BULK_STARTS[1])

    all_but_one(rs1_recv, 0).wait_recv()
    received = rs1_recv[...].astype(F32)
    outs, stats = received[:, :8], received[:, 8:]
    query = own_query[...]
    later = lax.rem(me, 4) >= 2
    fresh_scores = []
    for u in range(2):
        score = jnp.sum(query * own_fresh[u, :, :HD], axis=1, keepdims=True) * SCALE
        fresh_scores.append(score if u == 0 else jnp.where(later, score, NEG_FILL))
    top = jnp.max(stats, axis=0)[:, :1]
    top = jnp.maximum(top, jnp.maximum(fresh_scores[0], fresh_scores[1]))
    factor = jnp.exp(stats[:, :, :1] - top[None])
    weighted = jnp.sum(outs * factor, axis=0)
    totals = jnp.sum(stats * factor, axis=0)
    total = totals[:, 32:33] + totals[:, 64:65]
    for u in range(2):
        weight = jnp.exp(fresh_scores[u] - top)
        total = total + weight
        weighted = weighted + weight.astype(BF16).astype(F32) * own_fresh[u, :, HD:]
    part = (weighted / total).astype(BF16)
    ag1_send[...] = part
    ag1_recv[me] = part
    each_peer(lambda s, h: remote(ag1_send, ag1_recv.at[me], 1, s, h).start())
    start_bulk(BULK_STARTS[2])

    select = [
        jnp.where(iota((32, HD), 1) == iota((32, HD), 0) + q * 32, 1.0, 0.0) for q in range(4)
    ]
    weight_copies[0].wait()
    all_but_one(ag1_recv, 1).wait_recv()
    rows = ag1_recv[...].astype(F32).reshape(HQ, ROWS, HD)
    for a in range(HQ):
        attended[:, a * HD : (a + 1) * HD] = rows[a].astype(BF16)
    middle = hidden[...].astype(F32) + dot(attended[...], wo[...])
    scaled = middle * gain[...].astype(F32)
    lane32 = iota((ROWS, 32), 1)
    sums = dot(scaled, router[...].astype(F32), HIGHEST)
    square = jnp.sum(middle * middle, axis=1, keepdims=True)
    sums = jnp.where((lane32 == 0) | (lane32 == 16), square, sums)
    sums_high = sums.astype(BF16).astype(F32)
    sums = jnp.where(lane32 < 16, sums_high, sums - sums_high)

    def packed_rows(block, precision=None):
        return sum(
            dot(block[q * 8 : q * 8 + 8], select[q].astype(block.dtype), precision)
            for q in range(4)
        )

    part = jnp.concatenate(
        [packed_rows(scaled.astype(BF16)), packed_rows(sums.astype(BF16))], axis=0
    ).astype(BF16)
    ag2_send[...] = part
    ag2_recv[me] = part
    each_peer(lambda s, h: remote(ag2_send, ag2_recv.at[me], 2, s, h).start())
    start_bulk(BULK_STARTS[3])
    middle_packed = packed_rows(middle, HIGHEST)

    spread_row, spread_col = iota((HD, 512), 0), iota((HD, 512), 1)

    def spread(j):
        wanted = (spread_row // 32) * HD + j * 32 + lax.rem(spread_row, 32)
        return jnp.where(spread_col == wanted, 1.0, 0.0).astype(BF16)

    spreads = [spread(j) for j in range(4)]
    for copy in weight_copies[1:]:
        copy.wait()
    all_but_one(ag2_recv, 2).wait_recv()
    received = ag2_recv[...].astype(F32)
    blocks = received[:, :8].reshape(32, 4, 8, HD)
    ordered = sum(
        dot(blocks[:, j].reshape(256, HD).astype(BF16), spreads[j]) for j in range(4)
    )
    for n in range(32):
        features[:, n * HD : (n + 1) * HD] = jnp.concatenate(
            [ordered[n * 8 : n * 8 + 8, q * HD : (q + 1) * HD] for q in range(4)], axis=0
        ).astype(BF16)
    sums = jnp.sum(received[:, 8:], axis=0)
    fold_row, fold_col = iota((HD, HD), 0), iota((HD, HD), 1)
    folded = jnp.concatenate(
        [
            dot(
                sums,
                jnp.where(
                    (fold_row // 32 == q) & (lax.rem(fold_row, 16) == fold_col), 1.0, 0.0
                ),
                HIGHEST,
            )
            for q in range(4)
        ],
        axis=0,
    )
    inverse_rms = lax.rsqrt(folded[:, :1] / D + EPSILON)
    logits = folded * inverse_rms
    chosen = routes[...]
    first, second = chosen[:, :1], chosen[:, 1:2]
    expert_lane = iota((ROWS, HD), 1) - 1
    first_logit = jnp.sum(jnp.where(expert_lane == first, logits, 0.0), axis=1, keepdims=True)
    second_logit = jnp.sum(jnp.where(expert_lane == second, logits, 0.0), axis=1, keepdims=True)
    share = jnp.where(
        first == seq,
        1.0 / (1.0 + jnp.exp(second_logit - first_logit)),
        jnp.where(second == seq, 1.0 / (1.0 + jnp.exp(first_logit - second_logit)), 0.0),
    )
    gate = dot(features[...], wg[...]) * inverse_rms
    upward = dot(features[...], wu[...]) * inverse_rms
    inner = (gate / (1.0 + jnp.exp(-gate)) * upward).astype(BF16)
    start_bulk(BULK_STARTS[4])

    collect_row, collect_col = iota((HD, 512), 0), iota((HD, 512), 1)

    def collect(q):
        wanted = (collect_row // 32) * HD + q * 32 + lax.rem(collect_row, 32)
        return jnp.where(collect_col == wanted, 1.0, 0.0).astype(BF16)

    collects = [collect(q) for q in range(4)]
    produced = dot(inner, wd[...]) * share
    parts = sum(
        dot(
            jnp.concatenate(
                [produced[q * 8 : q * 8 + 8, n * HD : (n + 1) * HD] for n in range(32)], axis=0
            ).astype(BF16),
            collects[q],
        )
        for q in range(4)
    )
    for j in range(4):
        rs2_send[:, j] = parts[:, j * HD : (j + 1) * HD].reshape(32, 8, HD).astype(BF16)
    rs2_recv[me] = rs2_send[me // 4, lax.rem(me, 4)]

    def send_sums(to_seq, to_head):
        slot = to_seq * N_HEAD + to_head
        remote(
            rs2_send.at[slot // 4, lax.rem(slot, 4)], rs2_recv.at[me], 3, to_seq, to_head
        ).start()

    each_peer(send_sums)
    start_bulk(BULK_STARTS[5])
    all_but_one(rs2_recv, 3).wait_recv()
    mixed[...] = (middle_packed + jnp.sum(rs2_recv[...].astype(F32), axis=0)).astype(BF16)

    for buffer, phase in ((rs1_recv, 0), (ag1_recv, 1), (ag2_recv, 2), (rs2_recv, 3)):
        all_but_one(buffer, phase).wait_send()
    own_slot.wait()
    all_but_one(arrived, 4).wait_recv()
    all_but_one(arrived, 4).wait_send()


def body(
    lengths,
    page_owner,
    page_index,
    page_dest,
    src_cache,
    queries,
    new_kv,
    hidden_in,
    out_weight,
    norm_gain,
    router,
    routes,
    w_gate,
    w_up,
    w_down,
):
    seq = lax.axis_index("seq")
    head = lax.axis_index("head")
    me = seq * N_HEAD + head
    query_head, row_block = me // 4, me % 4
    own_query = lax.dynamic_slice(
        queries.reshape(ROWS, HQ * HD), (row_block * 8, query_head * HD), (8, HD)
    ).astype(F32)
    own_fresh = lax.dynamic_slice(
        new_kv, (0, row_block % 2 * 8, query_head // GROUP, 0), (2, 8, 1, 2 * HD)
    )[:, :, 0].astype(F32)
    wide_router = jnp.zeros((32, 32), F32)
    wide_router = wide_router.at[:, 1:9].set(router.astype(F32))
    wide_router = wide_router.at[:, 17:25].set(router.astype(F32))
    vmem = pl.BlockSpec(memory_space=pltpu.VMEM)
    smem = pl.BlockSpec(memory_space=pltpu.SMEM)
    hbm = pl.BlockSpec(memory_space=pl.ANY)
    arrived, mixed = pl.pallas_call(
        decode_kernel,
        out_shape=(
            jax.ShapeDtypeStruct((N_DEV, PAGE, 2 * HD), BF16),
            jax.ShapeDtypeStruct((8, HD), BF16),
        ),
        in_specs=[smem] * 4
        + [hbm, hbm, vmem, vmem, vmem, hbm, vmem, vmem, vmem, hbm, hbm, hbm],
        out_specs=(hbm, vmem),
        scratch_shapes=[
            pltpu.VMEM((PG_DEV, KVH, PAGE, 2 * HD), BF16),
            pltpu.VMEM((2 * N_SEQ, KVH, PAGE, 2 * HD), BF16),
            pltpu.VMEM((ROWS, D), BF16),
            pltpu.VMEM((D, 32), BF16),
            pltpu.VMEM((D, FF_DEV), BF16),
            pltpu.VMEM((D, FF_DEV), BF16),
            pltpu.VMEM((FF_DEV, D), BF16),
            pltpu.VMEM((N_DEV, 16, HD), BF16),
            pltpu.VMEM((N_DEV, 16, HD), BF16),
            pltpu.VMEM((8, HD), BF16),
            pltpu.VMEM((N_DEV, 8, HD), BF16),
            pltpu.VMEM((ROWS, D), BF16),
            pltpu.VMEM((16, HD), BF16),
            pltpu.VMEM((N_DEV, 16, HD), BF16),
            pltpu.VMEM((ROWS, D), BF16),
            pltpu.VMEM((32, 4, 8, HD), BF16),
            pltpu.VMEM((N_DEV, 8, HD), BF16),
            pltpu.SemaphoreType.DMA((N_SEQ,)),
            pltpu.SemaphoreType.DMA,
            pltpu.SemaphoreType.DMA((4,)),
            pltpu.SemaphoreType.DMA,
            pltpu.SemaphoreType.DMA((5,)),
            pltpu.SemaphoreType.DMA((5,)),
        ],
        compiler_params=pltpu.CompilerParams(
            collective_id=0, has_side_effects=True, vmem_limit_bytes=58 * 1024 * 1024
        ),
        name="decode",
    )(
        lengths,
        page_owner,
        page_index,
        page_dest,
        src_cache,
        queries.reshape(ROWS, HQ * HD),
        own_query,
        own_fresh,
        hidden_in.reshape(ROWS, 32),
        out_weight,
        norm_gain.reshape(1, 32),
        wide_router,
        routes.reshape(ROWS, 2),
        w_gate[0],
        w_up[0],
        w_down[0],
    )
    mixed = mixed.reshape(8, 4, 32).transpose(1, 0, 2).reshape(2, REQS, 32)
    first_slot = (head % 2) * SLOTS + seq * SLOTS_DEV
    slot_ids = first_slot + jnp.arange(SLOTS_DEV, dtype=jnp.int32)
    sources = jnp.arange(page_dest.shape[0], dtype=jnp.int32) // PG_DEV
    chosen = jnp.sum(
        jnp.where(page_dest[None, :] == slot_ids[:, None], sources[None, :], 0), axis=1
    )
    page_pool = jnp.take(arrived, chosen, axis=0)
    return (page_pool[None], mixed)


def solution(mesh):
    in_specs = (
        P(),
        P(),
        P(),
        P(),
        P(SEQ_HEAD, None, None, None),
        P(),
        P(),
        P(None, None, SEQ_HEAD),
        P(None, SEQ_HEAD),
        P(SEQ_HEAD),
        P(SEQ_HEAD, None),
        P(),
        P("seq", None, "head"),
        P("seq", None, "head"),
        P("seq", "head", None),
    )
    out_specs = (P("head", "seq", None, None), P(None, None, SEQ_HEAD))
    return jax.shard_map(body, mesh=mesh, in_specs=in_specs, out_specs=out_specs, check_vma=False)
```

time: 611 us -> 105 us (0.17)
  waiting for transfers between devices: 279 us -> 0 us
  blocking collectives: 208 us -> 0 us
  Pallas kernels: 0 us -> 87.7 us
  local copies, waits for them, and re-layouts: 42 us -> 8.47 us
  other arithmetic: 29.7 us -> 7.54 us
  matrix products: 18.5 us -> 0 us
  between operations: 14.7 us -> 0.73 us
  starting transfers between devices: 12.6 us -> 0 us
    reduce_scatter x12 -> x0, waiting for transfers between devices: 203 us -> none  [own_block(): blocks = lax.psum_scatter(blocks, axes[k], scatter_dimension=0, tiled=True)]
    all_gather x9 -> x0, blocking collectives: 126 us -> none  [the longest x8 64 us: joined_all(): pieces = jax.tree.map(lambda part: lax.all_gather(part, axis), array)]
    pallas_call x0 -> x1, Pallas kernels: none -> 87.7 us  [body(): pl.pallas_call(decode_kernel, out_shape=(jax.ShapeDtypeStruct((N_DEV, PAG...]
    unnamed x4 -> x0, blocking collectives: 46.5 us -> none
    all_to_all x1 -> x0, waiting for transfers between devices: 39.2 us -> none  [body(): lax.all_to_all(packed.reshape(device_count, capacity, PAGE, 2 * HD), SEQ_...]
    all_gather x4 -> x0, waiting for transfers between devices: 35.8 us -> none  [joined_all(): pieces = jax.tree.map(lambda part: lax.all_gather(part, axis), array)]
    psum x4 -> x0, blocking collectives: 35.6 us -> none  [over_axes(): array = lax.psum(array, axis)]
    dot_general x10 -> x0, matrix products: 18.5 us -> none  [the longest x1 5.12 us: body(): jnp.einsum('erf,efd->erd', inner_act, w_down, preferred_element_type=jnp....]
  transfers between devices with their start and end apart: 17 -> 0, of which waited for: 15 -> 0; matrix products, arithmetic and copies ran while one was open for 6% -> 0% of each run, Pallas kernels for 0% -> 0%
where the time goes in v1:
time: 105 us; the launch traced here: 104 us
  Pallas kernels  87.7 us (84%)
  local copies, waits for them, and re-layouts  8.47 us (8%)
  other arithmetic  7.54 us (7%)
    pallas_call x1, Pallas kernels, body(): pl.pallas_call(decode_kernel, out_shape=(jax.ShapeDtypeStruct((N_DEV, PAG...  87.7 us
    unnamed x8, local copies, waits for them, and re-layouts  3.05 us
    gather x1, local copies, waits for them, and re-layouts, body(): page_pool = jnp.take(arrived, chosen, axis=0)  2.98 us
    another operation x3, other arithmetic  2.7 us

profile of v1, /device:TPU:1, one launch (start us, length us, event | category | flops | bytes accessed | tf_op | source)
XLA Modules:
  0.0 104.5 jit_solution(3365966454136833605)
XLA Ops:
  0.6 0.0 copy-start
  0.6 0.7 compare_reduce_fusion.1
  1.4 0.6 compare_reduce_fusion
  2.0 1.3 %dynamic-slice_convert_fusion.own_query = f32[8,128]{1,0:T(8,128)} fusion(bf16[32,4096]{1,0:T(8,128)(2,1)} %bitcast.23, s32[]{:T(128)S(6)} %select_n.79, s32[]{:T(128)S(6)} %select_n.81), kind=kLoop, calls=%fused_computation.17 | loop fusion | flops 1024 | bytes 6152 | tf_op jit(solution)/shard_map/convert_element_type | solution.py:418
  3.3 0.8 copy.24
  4.1 0.9 select_reduce_fusion
  5.0 0.0 copy-done
  5.1 0.6 fusion.2.own_fresh
  5.7 1.4 %copy.29 = s32[2,16,2]{2,1,0:T(8,128)} copy(s32[2,16,2]{1,2,0:T(2,128)} %param.30) | data formatting | bytes 512 | tf_op jit(solution)/shard_map/reshape | solution.py:479
  7.0 1.3 %convert_select_fusion = (f32[32,8]{1,0:T(8,128)S(1)}, f32[32,8]{1,0:T(8,128)S(1)}) fusion(bf16[32,8]{1,0:T(8,128)(2,1)S(1)} %copy.24, pred[]{:T(512)} %compare_reduce_fusion, pred[]{:T(512)} %compare_reduce_fusion.1), kind=kLoop, calls=%fused_computation.3 | loop fusion | flops 768 | bytes 2562 | tf_op jit(solution)/shard_map/select.3
  8.4 0.1 scatter.6
  8.5 0.3 scatter.9.router
  8.8 0.0 copy-start.1
  8.8 2.3 %copy.26.wo_hbm = bf16[4096,32]{1,0:T(8,128)(2,1)} copy(bf16[4096,32]{0,1:T(8,128)(2,1)} %param.27) | data formatting | bytes 524288 | tf_op args[8]
  11.0 0.0 copy-done.1
  11.0 87.7 %decode.1 = (bf16[128,64,256]{2,1,0:T(8,128)(2,1)}, bf16[8,128]{1,0:T(8,128)(2,1)}) custom-call(s32[16]{0:T(128)} %lengths.1, s32[1536]{0:T(1024)} %page_owner.1, s32[1536]{0:T(1024)} %page_index.1, s32[1536]{0:T(1024)} %page_dest.1, bf16[12,8,64,256]{3,2,1,0:T(8,128)(2,1)} %src_hbm.1, bf16[32,4096]{1,0:T(8,128)(2,1)} %bitcast.24, ...), custom_call_target="tpu_custom_call" | custom-call | tf_op jit(solution)/shard_map/decode/pallas_call | solution.py:428
  98.8 3.0 %gather_fusion = bf16[96,64,256]{2,1,0:T(8,128)(2,1)S(1)} fusion(bf16[128,64,256]{2,1,0:T(8,128)(2,1)} %get-tuple-element.28, s32[1024]{0:T(1024)S(1)} %pad_clamp_fusion), kind=kCustom, calls=%fused_computation | custom fusion | bytes 6291840 | tf_op jit(solution)/shard_map/jit(_take)/gather | solution.py:491
  101.8 0.0 copy-start.2
  101.8 2.0 %bitcast_select_fusion = bf16[1,96,64,256]{3,2,1,0:T(8,128)(2,1)} fusion(bf16[96,64,256]{2,1,0:T(8,128)(2,1)S(1)} %gather_fusion, pred[96]{0:T(512)(128)(4,1)S(1)} %compare_and_fusion), kind=kLoop, calls=%fused_computation.1 | loop fusion | flops 1572864 | bytes 6291552 | tf_op jit(solution)/shard_map/jit(_take)/select_n | solution.py:491
  103.8 0.0 copy-done.2
  103.8 0.1 reshape.119
  103.9 0.6 copy.28
  (6 shorter events, 0.1 us)
Async XLA Ops:
  0.6 4.4 %copy-start = (bf16[2,16,8,256]{3,2,1,0:T(8,128)(2,1)S(1)}, bf16[2,16,8,256]{3,2,1,0:T(8,128)(2,1)}, u32[]{:S(2)}) copy-start(bf16[2,16,8,256]{3,2,1,0:T(8,128)(2,1)} %param.25) | copy-start | bytes 393220
  8.8 2.3 %copy-start.1 = (f32[32,32]{1,0:T(8,128)}, f32[32,32]{1,0:T(8,128)S(1)}, u32[]{:S(2)}) copy-start(f32[32,32]{1,0:T(8,128)S(1)} %scatter.9.router) | copy-start | bytes 12292
  101.8 2.0 %copy-start.2 = (bf16[8,128]{1,0:T(8,128)(2,1)S(1)}, bf16[8,128]{1,0:T(8,128)(2,1)}, u32[]{:S(2)}) copy-start(bf16[8,128]{1,0:T(8,128)(2,1)} %get-tuple-element.29) | copy-start | bytes 6148

commit v2 on v1

v2 whole, which is shorter than its diff:
```python
import functools

import jax
import jax.numpy as jnp
from jax import lax
from jax.experimental import pallas as pl
from jax.experimental.pallas import tpu as pltpu
from jax.sharding import PartitionSpec as P

D = 4096
HQ = 32
KVH = 8
GROUP = HQ // KVH
HD = 128
EXPERTS = 8
PAGE = 64
REQS = 16
ROWS = 32
FF_DEV = 512
PG_DEV = 12
SLOTS = 768
SLOTS_DEV = 96
N_SEQ = 8
N_HEAD = 16
N_DEV = N_SEQ * N_HEAD
NEG_FILL = -1e30
EPSILON = 1e-05
HIGHEST = lax.Precision.HIGHEST
SCALE = HD ** (-0.5)
SEQ_HEAD = ("seq", "head")
BF16 = jnp.bfloat16
F32 = jnp.float32
N_PLANE = 4
BULK_STARTS = ((14, 0), (14, 4), (14, 4), (5, 0), (14, 4), (4, 0), (14, 0), (48, 0))
MERGE, GATHER_A, FORWARD_A, GATHER_B, FORWARD_B, PAIR_SUMS, SUMS, BULK = range(4, 12)


def farthest_first(offsets):
    return sorted(offsets, key=lambda o: -sum(min(d, 4 - d) for d in o))


def balanced_order():
    left = [(n // 32, n // 16 % 2, n // 4 % 4, n % 4) for n in range(1, N_DEV)]
    loads, order = [0.0] * 6, []

    def added(offset):
        new = list(loads)
        for axis, d in enumerate((offset[2], offset[3], offset[0])):
            for way, amount in enumerate(((0, 1, 1, 0), (0, 0, 1, 1))):
                new[2 * axis + way] += amount[d]
        return new

    def spread(offset):
        new = added(offset)
        mean = sum(new) / 6
        return sum((n - mean) ** 2 for n in new), -sum(new)

    while left:
        best = min(left, key=spread)
        loads = added(best)
        left.remove(best)
        order.append(best)
    return order


PAGE_ORDER = balanced_order()
PLANE_OFFSETS = farthest_first([(n // 16, n // 4 % 4, n % 4) for n in range(1, 64)])


def iota(shape, dim):
    return lax.broadcasted_iota(jnp.int32, shape, dim)


def dot(a, b, precision=None):
    return jnp.dot(a, b, preferred_element_type=F32, precision=precision)


def decode_kernel(
    lengths,
    page_owner,
    page_index,
    page_dest,
    all_dests,
    src_hbm,
    queries_hbm,
    new_kv,
    hidden,
    wo_hbm,
    gain,
    router,
    routes,
    wg_hbm,
    wu_hbm,
    wd_hbm,
    arrived,
    mixed,
    chosen,
    src,
    packed,
    queries,
    wo,
    wg,
    wu,
    wd,
    rs1_send,
    rs1_pair,
    rs1_recv,
    ag1_send,
    ag1_recv,
    attended,
    ag2_send,
    ag2_recv,
    features,
    rs2_out,
    rs2_pair,
    rs2_send,
    rs2_recv,
    src_sem,
    query_sem,
    weight_sem,
    page_sem,
    send_sem,
    recv_sem,
):
    seq = lax.axis_index("seq")
    head = lax.axis_index("head")
    me = seq * N_HEAD + head
    heads = [lax.rem(head + u, N_HEAD) for u in range(N_HEAD)]
    z, core, x, y = seq // 2, lax.rem(seq, 2), head // 4, lax.rem(head, 4)
    zs = [lax.rem(z + t, 4) for t in range(4)]
    cores = [lax.rem(core + t, 2) for t in range(2)]
    xs = [lax.rem(x + t, 4) for t in range(4)]
    ys = [lax.rem(y + t, 4) for t in range(4)]
    other = 1 - core
    kv_heads = [2 * zs[t] + other for t in range(N_PLANE)] + [2 * zs[t] + core for t in range(N_PLANE)]

    def page_copy(t):
        return pltpu.make_async_copy(
            src_hbm.at[:, kv_heads[t]], src.at[:, kv_heads[t]], src_sem.at[t]
        )

    query_copy = pltpu.make_async_copy(queries_hbm, queries, query_sem)
    weight_copies = [
        pltpu.make_async_copy(a, b, weight_sem.at[n])
        for n, (a, b) in enumerate(((wo_hbm, wo), (wg_hbm, wg), (wu_hbm, wu), (wd_hbm, wd)))
    ]
    barrier = pltpu.get_barrier_semaphore()

    @jax.named_scope("greet")
    def each_peer(act):
        for dz, dx, dy in PLANE_OFFSETS:
            for to_core in (other, core):
                act(2 * zs[dz] + to_core, 4 * xs[dx] + ys[dy])
        act(2 * z + other, head)

    @jax.named_scope("each_plane")
    def each_of_core(act):
        for dz, dx, dy in PLANE_OFFSETS:
            act(zs[dz], 4 * xs[dx] + ys[dy])

    def greet(to_seq, to_head):
        pl.semaphore_signal(
            barrier,
            inc=1,
            device_id=(to_seq, to_head),
            device_id_type=pl.DeviceIdType.MESH,
        )

    for t in range(N_SEQ):
        page_copy(t).start()
    query_copy.start()
    each_peer(greet)

    def remote(source, target, phase, to_seq, to_head):
        return pltpu.make_async_remote_copy(
            src_ref=source,
            dst_ref=target,
            send_sem=send_sem.at[phase],
            recv_sem=recv_sem.at[phase],
            device_id=(to_seq, to_head),
            device_id_type=pl.DeviceIdType.MESH,
        )

    def to_other_core(source, target, phase):
        return remote(source, target, phase, 2 * z + other, head)

    def received_all(rest, phase):
        return remote(rest, rest, phase, 2 * z + other, head)

    def arrive(rest, phase):
        with jax.named_scope(f"arrive{phase}"):
            received_all(rest, phase).wait_recv()

    lane = iota((1, PG_DEV * PAGE), 1)
    token_owner = jnp.full((1, PG_DEV * PAGE), REQS, jnp.int32)
    for p in range(PG_DEV):
        owner = page_owner[me * PG_DEV + p]
        limit = lengths[jnp.minimum(owner, REQS - 1)] - page_index[me * PG_DEV + p] * PAGE
        inside = (lane >= p * PAGE) & (lane < p * PAGE + jnp.minimum(limit, PAGE))
        token_owner = jnp.where(inside, owner, token_owner)

    @jax.named_scope("pack")
    def pack_pages():
        groups = []
        for p in range(PG_DEV):
            dest = page_dest[me * PG_DEV + p]
            upper = jnp.where(dest >= SLOTS, 1, 0)
            within = dest - upper * SLOTS
            target = jnp.int32(0)
            for n in range(1, N_SEQ):
                target = target + jnp.where(within >= n * SLOTS_DEV, 2, 0)
            groups.append(target + upper)

        def one(group, carry):
            page = jnp.int32(0)
            for p in range(PG_DEV):
                page = jnp.where(groups[p] == group, p, page)
            for k in range(KVH):
                packed[group, k] = src[page, k]
            return carry

        lax.fori_loop(0, 2 * N_SEQ, one, 0)

    started, finished = [0], [0]

    def page_send(i):
        dz, dc, dx, dy = PAGE_ORDER[i]
        to_seq = zs[dz] * 2 + cores[dc]
        to_head = xs[dx] * 4 + ys[dy]
        part = packed.at[to_seq * 2 + lax.rem(to_head, 2), to_head // 2]
        return pltpu.make_async_remote_copy(
            src_ref=part,
            dst_ref=arrived.at[me],
            send_sem=page_sem.at[i],
            recv_sem=recv_sem.at[BULK],
            device_id=(to_seq, to_head),
            device_id_type=pl.DeviceIdType.MESH,
        )

    def finish_pages(count):
        while finished[0] < count:
            page_send(finished[0]).wait_send()
            finished[0] += 1

    @jax.named_scope("bulk")
    def start_bulk(point):
        count, window = BULK_STARTS[point]
        for i in range(started[0], started[0] + count):
            if window:
                finish_pages(i + 1 - window)
            page_send(i).start()
        started[0] += count

    row_request = lax.rem(iota((4 * ROWS, 1), 0), REQS)
    live = token_owner == row_request
    lane128 = iota((4 * ROWS, HD), 1)
    with jax.named_scope("pages"):
        for t in range(N_SEQ):
            page_copy(t).wait()
    query_copy.wait()
    for copy in weight_copies:
        copy.start()
    pack_pages()
    with jax.named_scope("greeted"):
        pl.semaphore_wait(barrier, N_DEV - 1)
    arrived[me] = packed[seq * 2 + lax.rem(head, 2), head // 2]
    start_bulk(0)

    @jax.named_scope("attend")
    def attend_head(t):
        k = kv_heads[t]
        asked = jnp.concatenate(
            [
                queries[:, pl.ds(pl.multiple_of((k * GROUP + g) * HD, HD), HD)]
                for g in range(GROUP)
            ],
            axis=0,
        )
        keys = src[:, k, :, :HD].reshape(PG_DEV * PAGE, HD)
        values = src[:, k, :, HD:].reshape(PG_DEV * PAGE, HD)
        scores = (
            lax.dot_general(asked, keys, (((1,), (1,)), ((), ())), preferred_element_type=F32)
            * SCALE
        )
        scores = jnp.where(live, scores, NEG_FILL)
        top = jnp.max(scores, axis=1, keepdims=True)
        shift = jnp.where(top > -1e29, jnp.ceil(top * 0.25) * 4.0, NEG_FILL)
        weights = jnp.where(live, jnp.exp(scores - shift), 0.0)
        total = jnp.sum(weights, axis=1, keepdims=True)
        weighted = dot(weights.astype(BF16), values)
        if t >= N_PLANE:
            pair = rs1_pair.at[zs[t - N_PLANE]]
            arrive(pair, t - N_PLANE)
            pair = pair[...].astype(F32)
            pair_out = pair[:, :8].reshape(4 * ROWS, HD)
            pair_stats = pair[:, 8:].reshape(4 * ROWS, HD)
            pair_shift = pair_stats[:, :1]
            pair_total = pair_stats[:, 32:33] + pair_stats[:, 64:65]
            joint = jnp.maximum(shift, pair_shift)
            factor, pair_factor = jnp.exp(shift - joint), jnp.exp(pair_shift - joint)
            total = total * factor + pair_total * pair_factor
            weighted = weighted * factor + pair_out * pair_factor
            shift = joint
        total_high = total.astype(BF16).astype(F32)
        stats = jnp.where(
            lane128 < 32, shift, jnp.where(lane128 < 64, total_high, total - total_high)
        )
        rs1_send[k] = jnp.concatenate(
            [weighted.reshape(16, 8, HD), stats.reshape(16, 8, HD)], axis=1
        ).astype(BF16)

    for t in range(N_PLANE):
        attend_head(t)
        to_other_core(rs1_send.at[kv_heads[t]], rs1_pair.at[zs[t]], t).start()
    slot = z * N_HEAD + head
    for t in range(N_PLANE, N_SEQ):
        attend_head(t)
        for u in range(N_HEAD):
            part = rs1_send.at[kv_heads[t], heads[u]]
            if t > N_PLANE or u:
                remote(part, rs1_recv.at[slot], MERGE, kv_heads[t], heads[u]).start()
            else:
                rs1_recv[slot] = part[...]
    start_bulk(1)

    slot_row, slot_lane = iota((HD, HD), 0), iota((HD, HD), 1)
    wanted_slot = slot_row + lax.rem(head, 2) * SLOTS + seq * SLOTS_DEV
    found = jnp.zeros((HD, HD), jnp.int32)
    for n in range(N_DEV * PG_DEV // HD):
        origin = (n * HD + iota((1, HD), 1)) // PG_DEV
        found = found + jnp.where(all_dests[n : n + 1] == wanted_slot, origin, 0)
    found = jnp.sum(found.astype(F32), axis=1, keepdims=True)
    found = jnp.where(slot_row == slot_lane, found, 0.0)
    chosen[...] = jnp.sum(found, axis=0, keepdims=True).astype(jnp.int32)

    block = lax.rem(me, 4)
    later = block >= 2
    column = queries[:, pl.ds(pl.multiple_of(me // 4 * HD, HD), HD)].astype(F32)
    query = column[:8]
    for n in range(1, 4):
        query = jnp.where(block == n, column[n * 8 : n * 8 + 8], query)
    kv_lane = iota((8, KVH, 2 * HD), 1)
    first_request = lax.rem(block, 2) * 8
    own_fresh = [
        jnp.sum(
            jnp.where(
                kv_lane == me // 16,
                new_kv[u, pl.ds(first_request, 8)].astype(F32),
                0.0,
            ),
            axis=1,
        )
        for u in range(2)
    ]
    fresh_scores = []
    for u in range(2):
        score = jnp.sum(query * own_fresh[u][:, :HD], axis=1, keepdims=True) * SCALE
        fresh_scores.append(score if u == 0 else jnp.where(later, score, NEG_FILL))
    arrive(rs1_recv.at[pl.ds(0, N_DEV // 2 - 1)], MERGE)
    received = rs1_recv[...].astype(F32)
    outs, stats = received[:, :8], received[:, 8:]
    top = jnp.max(stats, axis=0)[:, :1]
    top = jnp.maximum(top, jnp.maximum(fresh_scores[0], fresh_scores[1]))
    factor = jnp.exp(stats[:, :, :1] - top[None])
    weighted = jnp.sum(outs * factor, axis=0)
    totals = jnp.sum(stats * factor, axis=0)
    total = totals[:, 32:33] + totals[:, 64:65]
    for u in range(2):
        weight = jnp.exp(fresh_scores[u] - top)
        total = total + weight
        weighted = weighted + weight.astype(BF16).astype(F32) * own_fresh[u][:, HD:]
    part = (weighted / total).astype(BF16)
    ag1_send[...] = part
    ag1_recv[core, slot] = part

    def gather(part, whole, phase):
        each_of_core(
            lambda to_z, to_head: remote(
                part, whole.at[core, slot], phase, 2 * to_z + core, to_head
            ).start()
        )

    gather(ag1_send, ag1_recv, GATHER_A)
    start_bulk(2)

    select = [
        jnp.where(iota((32, HD), 1) == iota((32, HD), 0) + q * 32, 1.0, 0.0) for q in range(4)
    ]
    router_row = iota((ROWS, EXPERTS), 0)
    wide_router = dot(
        jnp.where(lax.rem(router_row, 16) == iota((ROWS, EXPERTS), 1) + 1, 1.0, 0.0).astype(BF16),
        router[...],
    )
    weight_copies[0].wait()
    def forward(whole, phase, point):
        half = whole.at[core]
        arrive(half.at[pl.ds(0, N_DEV // 2 - 1)], phase)
        to_other_core(half, half, phase + 1).start()
        start_bulk(point)
        arrive(half, phase + 1)

    forward(ag1_recv, GATHER_A, 3)
    for n in range(N_PLANE):
        for c in range(2):
            rows = ag1_recv[c, n * N_HEAD : (n + 1) * N_HEAD].astype(F32).reshape(4, ROWS, HD)
            for g in range(GROUP):
                a = (n * 2 + c) * GROUP + g
                attended[:, a * HD : (a + 1) * HD] = rows[g].astype(BF16)
    middle = hidden[...].astype(F32) + lax.dot_general(
        attended[...], wo[...], (((1,), (1,)), ((), ())), preferred_element_type=F32
    )
    scaled = middle * gain[...].astype(F32)
    lane32 = iota((ROWS, 32), 1)
    sums = lax.dot_general(
        scaled,
        wide_router,
        (((1,), (1,)), ((), ())),
        preferred_element_type=F32,
        precision=HIGHEST,
    )
    square = jnp.sum(middle * middle, axis=1, keepdims=True)
    sums = jnp.where((lane32 == 0) | (lane32 == 16), square, sums)
    sums_high = sums.astype(BF16).astype(F32)
    sums = jnp.where(lane32 < 16, sums_high, sums - sums_high)

    def packed_rows(block, precision=None):
        return sum(
            dot(block[q * 8 : q * 8 + 8], select[q].astype(block.dtype), precision)
            for q in range(4)
        )

    part = jnp.concatenate(
        [packed_rows(scaled.astype(BF16)), packed_rows(sums.astype(BF16))], axis=0
    ).astype(BF16)
    ag2_send[...] = part
    ag2_recv[core, slot] = part
    gather(ag2_send, ag2_recv, GATHER_B)
    start_bulk(4)
    middle_packed = packed_rows(middle, HIGHEST)

    spread_row, spread_col = iota((HD, 512), 0), iota((HD, 512), 1)

    def spread(j):
        wanted = (spread_row // 32) * HD + j * 32 + lax.rem(spread_row, 32)
        return jnp.where(spread_col == wanted, 1.0, 0.0).astype(BF16)

    spreads = [spread(j) for j in range(4)]
    for copy in weight_copies[1:]:
        copy.wait()
    forward(ag2_recv, GATHER_B, 5)
    start_bulk(6)
    received = ag2_recv[...].astype(F32)
    blocks = received[:, :, :8].reshape(32, 4, 8, HD)
    ordered = sum(
        dot(blocks[:, j].reshape(256, HD).astype(BF16), spreads[j]) for j in range(4)
    )
    for n in range(32):
        place = n // 4 % 4 * 8 + n // 16 * 4 + n % 4
        features[:, place * HD : (place + 1) * HD] = jnp.concatenate(
            [ordered[n * 8 : n * 8 + 8, q * HD : (q + 1) * HD] for q in range(4)], axis=0
        ).astype(BF16)
    sums = jnp.sum(jnp.sum(received[:, :, 8:], axis=1), axis=0)
    fold_row, fold_col = iota((HD, HD), 0), iota((HD, HD), 1)
    folded = jnp.concatenate(
        [
            dot(
                sums,
                jnp.where(
                    (fold_row // 32 == q) & (lax.rem(fold_row, 16) == fold_col), 1.0, 0.0
                ),
                HIGHEST,
            )
            for q in range(4)
        ],
        axis=0,
    )
    inverse_rms = lax.rsqrt(folded[:, :1] / D + EPSILON)
    logits = folded * inverse_rms
    diagonal = iota((REQS, REQS), 0) == iota((REQS, REQS), 1)

    def picked(choice):
        rows = [
            jnp.sum(
                jnp.where(diagonal, routes[s, choice : choice + 1, :].astype(F32), 0.0),
                axis=1,
                keepdims=True,
            )
            for s in range(2)
        ]
        return jnp.concatenate(rows, axis=0).astype(jnp.int32)

    first, second = picked(0), picked(1)
    expert_lane = iota((ROWS, HD), 1) - 1
    first_logit = jnp.sum(jnp.where(expert_lane == first, logits, 0.0), axis=1, keepdims=True)
    second_logit = jnp.sum(jnp.where(expert_lane == second, logits, 0.0), axis=1, keepdims=True)
    share = jnp.where(
        first == seq,
        1.0 / (1.0 + jnp.exp(second_logit - first_logit)),
        jnp.where(second == seq, 1.0 / (1.0 + jnp.exp(first_logit - second_logit)), 0.0),
    )
    gate = dot(features[...], wg[...]) * inverse_rms
    upward = dot(features[...], wu[...]) * inverse_rms
    inner = (gate / (1.0 + jnp.exp(-gate)) * upward).astype(BF16)

    collect_row, collect_col = iota((HD, 512), 0), iota((HD, 512), 1)

    def collect(q):
        wanted = (collect_row // 32) * HD + q * 32 + lax.rem(collect_row, 32)
        return jnp.where(collect_col == wanted, 1.0, 0.0).astype(BF16)

    collects = [collect(q) for q in range(4)]
    def produce(parity):
        products = [
            dot(inner, wd[:, pl.ds(pl.multiple_of((2 * n + parity) * 512, 512), 512)]) * share
            for n in range(N_PLANE)
        ]
        return sum(
            dot(
                jnp.concatenate(
                    [
                        product[q * 8 : q * 8 + 8, n * HD : (n + 1) * HD]
                        for product in products
                        for n in range(4)
                    ],
                    axis=0,
                ).astype(BF16),
                collects[q],
            )
            for q in range(4)
        )

    with jax.named_scope("down"):
        parts = produce(other)
        for j in range(4):
            rs2_out[:, j] = parts[:, j * HD : (j + 1) * HD].reshape(16, 8, HD).astype(BF16)
        to_other_core(rs2_out, rs2_pair, PAIR_SUMS).start()
        parts = produce(core)
    arrive(rs2_pair, PAIR_SUMS)
    for j in range(4):
        part = parts[:, j * HD : (j + 1) * HD].reshape(16, 8, HD)
        rs2_send[:, j] = (part + rs2_pair[:, j].astype(F32)).astype(BF16)
    rs2_recv[slot] = rs2_send[slot // 4, lax.rem(slot, 4)]

    def send_sums(to_z, to_head):
        part = rs2_send.at[to_z * 4 + to_head // 4, lax.rem(to_head, 4)]
        remote(part, rs2_recv.at[slot], SUMS, 2 * to_z + core, to_head).start()

    each_of_core(send_sums)
    start_bulk(7)
    arrive(rs2_recv.at[pl.ds(0, N_DEV // 2 - 1)], SUMS)
    mixed[...] = (middle_packed + jnp.sum(rs2_recv[...].astype(F32), axis=0)).astype(BF16)

    most = N_DEV // 2 - 1
    for t in range(N_PLANE):
        received_all(rs1_pair.at[t], t).wait_send()
    for rest, phase in (
        (rs1_recv.at[pl.ds(0, most)], MERGE),
        (ag1_recv.at[0, pl.ds(0, most)], GATHER_A),
        (ag1_recv.at[0], FORWARD_A),
        (ag2_recv.at[0, pl.ds(0, most)], GATHER_B),
        (ag2_recv.at[0], FORWARD_B),
        (rs2_pair, PAIR_SUMS),
        (rs2_recv.at[pl.ds(0, most)], SUMS),
    ):
        received_all(rest, phase).wait_send()
    arrive(arrived.at[pl.ds(0, N_DEV - 1)], BULK)
    finish_pages(N_DEV - 1)


def place_kernel(chosen, arrived, mixed_packed, pool, mixed, sem):
    for j in range(SLOTS_DEV):
        pltpu.make_async_copy(arrived.at[chosen[0, j]], pool.at[j], sem).start()
    block = mixed_packed[...].astype(F32)
    for s in range(2):
        mixed[s] = jnp.concatenate(
            [block[:, q * 32 : (q + 1) * 32] for q in (2 * s, 2 * s + 1)], axis=0
        ).astype(BF16)
    pltpu.make_async_copy(arrived.at[pl.ds(0, SLOTS_DEV)], pool, sem).wait()


def body(
    lengths,
    page_owner,
    page_index,
    page_dest,
    src_cache,
    queries,
    new_kv,
    hidden_in,
    out_weight,
    norm_gain,
    router,
    routes,
    w_gate,
    w_up,
    w_down,
):
    vmem = pl.BlockSpec(memory_space=pltpu.VMEM)
    smem = pl.BlockSpec(memory_space=pltpu.SMEM)
    hbm = pl.BlockSpec(memory_space=pltpu.HBM)
    arrived, mixed, chosen = pl.pallas_call(
        decode_kernel,
        out_shape=(
            pltpu.VMEM((N_DEV, PAGE, 2 * HD), BF16),
            pltpu.VMEM((8, HD), BF16),
            pltpu.VMEM((1, HD), jnp.int32),
        ),
        in_specs=[smem] * 4
        + [vmem, hbm, hbm, vmem, vmem, hbm, vmem, vmem, vmem, hbm, hbm, hbm],
        out_specs=(vmem, vmem, vmem),
        scratch_shapes=[
            pltpu.VMEM((PG_DEV, KVH, PAGE, 2 * HD), BF16),
            pltpu.VMEM((2 * N_SEQ, KVH, PAGE, 2 * HD), BF16),
            pltpu.VMEM((ROWS, D), BF16),
            pltpu.VMEM((32, D), BF16),
            pltpu.VMEM((D, FF_DEV), BF16),
            pltpu.VMEM((D, FF_DEV), BF16),
            pltpu.VMEM((FF_DEV, D), BF16),
            pltpu.VMEM((KVH, 16, 16, HD), BF16),
            pltpu.VMEM((N_PLANE, 16, 16, HD), BF16),
            pltpu.VMEM((N_DEV // 2, 16, HD), BF16),
            pltpu.VMEM((8, HD), BF16),
            pltpu.VMEM((2, N_DEV // 2, 8, HD), BF16),
            pltpu.VMEM((ROWS, D), BF16),
            pltpu.VMEM((16, HD), BF16),
            pltpu.VMEM((2, N_DEV // 2, 16, HD), BF16),
            pltpu.VMEM((ROWS, D), BF16),
            pltpu.VMEM((16, 4, 8, HD), BF16),
            pltpu.VMEM((16, 4, 8, HD), BF16),
            pltpu.VMEM((16, 4, 8, HD), BF16),
            pltpu.VMEM((N_DEV // 2, 8, HD), BF16),
            pltpu.SemaphoreType.DMA((N_SEQ,)),
            pltpu.SemaphoreType.DMA,
            pltpu.SemaphoreType.DMA((4,)),
            pltpu.SemaphoreType.DMA((N_DEV - 1,)),
            pltpu.SemaphoreType.DMA((12,)),
            pltpu.SemaphoreType.DMA((12,)),
        ],
        compiler_params=pltpu.CompilerParams(
            collective_id=0, has_side_effects=True, vmem_limit_bytes=59 * 1024 * 1024
        ),
        name="decode",
    )(
        lengths,
        page_owner,
        page_index,
        page_dest,
        page_dest.reshape(N_DEV * PG_DEV // HD, HD),
        src_cache,
        queries.reshape(ROWS, HQ * HD),
        new_kv,
        hidden_in.reshape(ROWS, 32),
        out_weight.T,
        norm_gain.reshape(1, 32),
        router.T,
        routes.transpose(0, 2, 1),
        w_gate[0],
        w_up[0],
        w_down[0],
    )
    page_pool, mixed = pl.pallas_call(
        place_kernel,
        out_shape=(
            jax.ShapeDtypeStruct((SLOTS_DEV, PAGE, 2 * HD), BF16),
            jax.ShapeDtypeStruct((2, REQS, 32), BF16),
        ),
        in_specs=[smem, vmem, vmem],
        out_specs=(hbm, vmem),
        scratch_shapes=[pltpu.SemaphoreType.DMA],
        compiler_params=pltpu.CompilerParams(vmem_limit_bytes=1024 * 1024),
        name="place",
    )(
        chosen,
        pltpu.with_memory_space_constraint(arrived, pltpu.VMEM),
        pltpu.with_memory_space_constraint(mixed, pltpu.VMEM),
    )
    return (page_pool[None], mixed)


def solution(mesh):
    in_specs = (
        P(),
        P(),
        P(),
        P(),
        P(SEQ_HEAD, None, None, None),
        P(),
        P(),
        P(None, None, SEQ_HEAD),
        P(None, SEQ_HEAD),
        P(SEQ_HEAD),
        P(SEQ_HEAD, None),
        P(),
        P("seq", None, "head"),
        P("seq", None, "head"),
        P("seq", "head", None),
    )
    out_specs = (P("head", "seq", None, None), P(None, None, SEQ_HEAD))
    return jax.shard_map(body, mesh=mesh, in_specs=in_specs, out_specs=out_specs, check_vma=False)
```

time: 105 us -> 78.9 us (0.75)
  Pallas kernels: 87.7 us -> 78.1 us
  local copies, waits for them, and re-layouts: 8.47 us -> 0 us
  other arithmetic: 7.54 us -> 0 us
    pallas_call x1 -> x2, Pallas kernels: 87.7 us -> 78.1 us  [the longest x1 75.4 us: body(): pl.pallas_call(decode_kernel, out_shape=(pltpu.VMEM((N_DEV, PAGE, 2 * HD)...]
    unnamed x8 -> x0, local copies, waits for them, and re-layouts: 3.05 us -> none
    gather x1 -> x0, local copies, waits for them, and re-layouts: 2.98 us -> none  [body(): page_pool = jnp.take(arrived, chosen, axis=0)]
    another operation x3 -> x0, other arithmetic: 2.7 us -> none
    select_n x3 -> x0, other arithmetic: 2.03 us -> none  [the longest x2 2.02 us: body(): page_pool = jnp.take(arrived, chosen, axis=0)]
    convert_element_type x2 -> x0, other arithmetic: 1.87 us -> none  [the longest x1 1.27 us: body(): own_query = lax.dynamic_slice(queries.reshape(ROWS, HQ * HD), (row_block...]
    reshape x2 -> x0, local copies, waits for them, and re-layouts: 1.44 us -> none  [the longest x1 1.36 us: body(): routes.reshape(ROWS, 2)]
where the time goes in v2:
time: 78.9 us; the launch traced here: 78.8 us
  Pallas kernels  78.1 us (99%)
    pallas_call x1, Pallas kernels, body(): pl.pallas_call(decode_kernel, out_shape=(pltpu.VMEM((N_DEV, PAGE, 2 * HD)...  75.4 us
    pallas_call x1, Pallas kernels, body(): pl.pallas_call(place_kernel, out_shape=(jax.ShapeDtypeStruct((SLOTS_DEV,...  2.77 us

profile of v2, /device:TPU:1, one launch (start us, length us, event | category | flops | bytes accessed | tf_op | source)
XLA Modules:
  0.0 78.8 jit_solution(16266113480407182036)
XLA Ops:
  0.6 75.4 %decode.1 = (bf16[128,64,256]{2,1,0:T(8,128)(2,1)S(1)}, bf16[8,128]{1,0:T(8,128)(2,1)S(1)}, s32[1,128]{1,0:T(1,128)S(1)}) custom-call(s32[16]{0:T(128)} %lengths.1, s32[1536]{0:T(1024)} %page_owner.1, s32[1536]{0:T(1024)} %page_index.1, s32[1536]{0:T(1024)} %page_dest.1, s32[12,128]{1,0:T(8,128)} %bitcast.16, bf16[12,8,64,256]{3,2,1,0:T(8,128)(2,1)} %src_hbm.1, ...), custom_call_target="tpu_custom_call" | custom-call | tf_op jit(solution)/shard_map/decode/pallas_call | solution.py:601
  76.0 2.8 %place.1 = (bf16[96,64,256]{2,1,0:T(8,128)(2,1)}, bf16[2,16,32]{2,1,0:T(8,128)(2,1)}) custom-call(s32[1,128]{1,0:T(1,128)S(1)} %get-tuple-element.7.chosen, bf16[128,64,256]{2,1,0:T(8,128)(2,1)S(1)} %get-tuple-element.8.arrived, bf16[8,128]{1,0:T(8,128)(2,1)S(1)} %get-tuple-element.9.mixed_packed), custom_call_target="tpu_custom_call" | custom-call | tf_op jit(solution)/shard_map/place/pallas_call | solution.py:661

commit v3 on v2

--- a/solution.py
+++ b/solution.py
@@ -31,7 +31,8 @@
 BF16 = jnp.bfloat16
 F32 = jnp.float32
 N_PLANE = 4
-BULK_STARTS = ((14, 0), (14, 4), (14, 4), (5, 0), (14, 4), (4, 0), (14, 0), (48, 0))
+PACED = 4
+BULK_STARTS = ((14, 0), (14, 1), (14, 1), (5, 0), (14, 1), (4, 0), (28, 0), (34, 0))
 MERGE, GATHER_A, FORWARD_A, GATHER_B, FORWARD_B, PAIR_SUMS, SUMS, BULK = range(4, 12)
 
 
@@ -76,25 +77,37 @@
 
 
 def decode_kernel(
+    lengths_hbm,
+    page_owner_hbm,
+    page_index_hbm,
+    page_dest_hbm,
+    all_dests_hbm,
+    src_hbm,
+    queries_hbm,
+    new_kv_hbm,
+    hidden_hbm,
+    wo_hbm,
+    gain_hbm,
+    router_hbm,
+    routes_hbm,
+    wg_hbm,
+    wu_hbm,
+    wd_hbm,
+    pool,
+    mixed,
     lengths,
     page_owner,
     page_index,
     page_dest,
     all_dests,
-    src_hbm,
-    queries_hbm,
     new_kv,
     hidden,
-    wo_hbm,
     gain,
     router,
     routes,
-    wg_hbm,
-    wu_hbm,
-    wd_hbm,
+    chosen,
+    chosen_scalars,
     arrived,
-    mixed,
-    chosen,
     src,
     packed,
     queries,
@@ -115,6 +128,8 @@
     rs2_pair,
     rs2_send,
     rs2_recv,
+    small_sem,
+    chosen_sem,
     src_sem,
     query_sem,
     weight_sem,
@@ -166,10 +181,32 @@
             device_id_type=pl.DeviceIdType.MESH,
         )
 
+    small_copies = [
+        pltpu.make_async_copy(a, b, small_sem.at[n])
+        for n, (a, b) in enumerate(
+            (
+                (lengths_hbm, lengths),
+                (page_owner_hbm, page_owner),
+                (page_index_hbm, page_index),
+                (page_dest_hbm, page_dest),
+                (all_dests_hbm, all_dests),
+                (new_kv_hbm, new_kv),
+                (hidden_hbm, hidden),
+                (gain_hbm, gain),
+                (router_hbm, router),
+                (routes_hbm, routes),
+            )
+        )
+    ]
     for t in range(N_SEQ):
         page_copy(t).start()
+    for copy in small_copies:
+        copy.start()
     query_copy.start()
     each_peer(greet)
+    with jax.named_scope("small"):
+        for copy in small_copies:
+            copy.wait()
 
     def remote(source, target, phase, to_seq, to_head):
         return pltpu.make_async_remote_copy(
@@ -221,9 +258,9 @@
 
         lax.fori_loop(0, 2 * N_SEQ, one, 0)
 
-    started, finished = [0], [0]
-
-    def page_send(i):
+    started, paced = [0], []
+
+    def page_send(i, sem):
         dz, dc, dx, dy = PAGE_ORDER[i]
         to_seq = zs[dz] * 2 + cores[dc]
         to_head = xs[dx] * 4 + ys[dy]
@@ -231,25 +268,39 @@
         return pltpu.make_async_remote_copy(
             src_ref=part,
             dst_ref=arrived.at[me],
-            send_sem=page_sem.at[i],
+            send_sem=page_sem.at[sem],
             recv_sem=recv_sem.at[BULK],
             device_id=(to_seq, to_head),
             device_id_type=pl.DeviceIdType.MESH,
         )
-
-    def finish_pages(count):
-        while finished[0] < count:
-            page_send(finished[0]).wait_send()
-            finished[0] += 1
 
     @jax.named_scope("bulk")
     def start_bulk(point):
         count, window = BULK_STARTS[point]
         for i in range(started[0], started[0] + count):
+            sem = PACED + point
             if window:
-                finish_pages(i + 1 - window)
-            page_send(i).start()
+                sem = len(paced) % PACED
+                if len(paced) >= PACED:
+                    page_send(*paced[-PACED]).wait_send()
+                paced.append((i, sem))
+            page_send(i, sem).start()
         started[0] += count
+
+    def finish_pages():
+        for i, sem in paced[-PACED:]:
+            page_send(i, sem).wait_send()
+        for point, (count, window) in enumerate(BULK_STARTS):
+            if not window:
+                rest = arrived.at[pl.ds(0, count)]
+                pltpu.make_async_remote_copy(
+                    src_ref=rest,
+                    dst_ref=rest,
+                    send_sem=page_sem.at[PACED + point],
+                    recv_sem=recv_sem.at[BULK],
+                    device_id=(2 * z + other, head),
+                    device_id_type=pl.DeviceIdType.MESH,
+                ).wait_send()
 
     row_request = lax.rem(iota((4 * ROWS, 1), 0), REQS)
     live = token_owner == row_request
@@ -332,6 +383,8 @@
     found = jnp.sum(found.astype(F32), axis=1, keepdims=True)
     found = jnp.where(slot_row == slot_lane, found, 0.0)
     chosen[...] = jnp.sum(found, axis=0, keepdims=True).astype(jnp.int32)
+    chosen_copy = pltpu.make_async_copy(chosen, chosen_scalars, chosen_sem)
+    chosen_copy.start()
 
     block = lax.rem(me, 4)
     later = block >= 2
@@ -548,7 +601,12 @@
     each_of_core(send_sums)
     start_bulk(7)
     arrive(rs2_recv.at[pl.ds(0, N_DEV // 2 - 1)], SUMS)
-    mixed[...] = (middle_packed + jnp.sum(rs2_recv[...].astype(F32), axis=0)).astype(BF16)
+    block = middle_packed + jnp.sum(rs2_recv[...].astype(F32), axis=0)
+    for s in range(2):
+        mixed[s] = jnp.concatenate(
+            [block[:, q * 32 : (q + 1) * 32] for q in (2 * s, 2 * s + 1)], axis=0
+        ).astype(BF16)
+    chosen_copy.wait()
 
     most = N_DEV // 2 - 1
     for t in range(N_PLANE):
@@ -564,18 +622,30 @@
     ):
         received_all(rest, phase).wait_send()
     arrive(arrived.at[pl.ds(0, N_DEV - 1)], BULK)
-    finish_pages(N_DEV - 1)
-
-
-def place_kernel(chosen, arrived, mixed_packed, pool, mixed, sem):
-    for j in range(SLOTS_DEV):
-        pltpu.make_async_copy(arrived.at[chosen[0, j]], pool.at[j], sem).start()
-    block = mixed_packed[...].astype(F32)
-    for s in range(2):
-        mixed[s] = jnp.concatenate(
-            [block[:, q * 32 : (q + 1) * 32] for q in (2 * s, 2 * s + 1)], axis=0
-        ).astype(BF16)
-    pltpu.make_async_copy(arrived.at[pl.ds(0, SLOTS_DEV)], pool, sem).wait()
+    finish_pages()
+    with jax.named_scope("place"):
+
+        def place(n, carry):
+            for j in range(8):
+                origin = jnp.clip(chosen_scalars[0, n * 8 + j], 0, N_DEV - 1)
+                pool[n * 8 + j] = arrived[origin]
+            return carry
+
+        lax.fori_loop(0, SLOTS_DEV // 8, place, 0)
+
+
+def finish_kernel(pool, mixed, pool_out, mixed_out, sem):
+    parts = [
+        pltpu.make_async_copy(
+            pool.at[pl.ds(n * 16, 16)], pool_out.at[pl.ds(n * 16, 16)], sem.at[n]
+        )
+        for n in range(6)
+    ]
+    parts.append(pltpu.make_async_copy(mixed, mixed_out, sem.at[6]))
+    for part in parts:
+        part.start()
+    for part in parts:
+        part.wait()
 
 
 def body(
@@ -596,19 +666,29 @@
     w_down,
 ):
     vmem = pl.BlockSpec(memory_space=pltpu.VMEM)
-    smem = pl.BlockSpec(memory_space=pltpu.SMEM)
     hbm = pl.BlockSpec(memory_space=pltpu.HBM)
-    arrived, mixed, chosen = pl.pallas_call(
+    page_pool, mixed = pl.pallas_call(
         decode_kernel,
         out_shape=(
+            pltpu.VMEM((SLOTS_DEV, PAGE, 2 * HD), BF16),
+            pltpu.VMEM((2, REQS, 32), BF16),
+        ),
+        in_specs=[hbm] * 16,
+        out_specs=(vmem, vmem),
+        scratch_shapes=[
+            pltpu.SMEM((REQS,), jnp.int32),
+            pltpu.SMEM((N_DEV * PG_DEV,), jnp.int32),
+            pltpu.SMEM((N_DEV * PG_DEV,), jnp.int32),
+            pltpu.SMEM((N_DEV * PG_DEV,), jnp.int32),
+            pltpu.VMEM((N_DEV * PG_DEV // HD, HD), jnp.int32),
+            pltpu.VMEM((2, REQS, KVH, 2 * HD), BF16),
+            pltpu.VMEM((ROWS, 32), BF16),
+            pltpu.VMEM((1, 32), BF16),
+            pltpu.VMEM((EXPERTS, 32), BF16),
+            pltpu.VMEM((2, 2, REQS), jnp.int32),
+            pltpu.VMEM((1, HD), jnp.int32),
+            pltpu.SMEM((1, HD), jnp.int32),
             pltpu.VMEM((N_DEV, PAGE, 2 * HD), BF16),
-            pltpu.VMEM((8, HD), BF16),
-            pltpu.VMEM((1, HD), jnp.int32),
-        ),
-        in_specs=[smem] * 4
-        + [vmem, hbm, hbm, vmem, vmem, hbm, vmem, vmem, vmem, hbm, hbm, hbm],
-        out_specs=(vmem, vmem, vmem),
-        scratch_shapes=[
             pltpu.VMEM((PG_DEV, KVH, PAGE, 2 * HD), BF16),
             pltpu.VMEM((2 * N_SEQ, KVH, PAGE, 2 * HD), BF16),
             pltpu.VMEM((ROWS, D), BF16),
@@ -629,15 +709,17 @@
             pltpu.VMEM((16, 4, 8, HD), BF16),
             pltpu.VMEM((16, 4, 8, HD), BF16),
             pltpu.VMEM((N_DEV // 2, 8, HD), BF16),
+            pltpu.SemaphoreType.DMA((10,)),
+            pltpu.SemaphoreType.DMA,
             pltpu.SemaphoreType.DMA((N_SEQ,)),
             pltpu.SemaphoreType.DMA,
             pltpu.SemaphoreType.DMA((4,)),
-            pltpu.SemaphoreType.DMA((N_DEV - 1,)),
+            pltpu.SemaphoreType.DMA((PACED + len(BULK_STARTS),)),
             pltpu.SemaphoreType.DMA((12,)),
             pltpu.SemaphoreType.DMA((12,)),
         ],
         compiler_params=pltpu.CompilerParams(
-            collective_id=0, has_side_effects=True, vmem_limit_bytes=59 * 1024 * 1024
+            collective_id=0, has_side_effects=True, vmem_limit_bytes=60 * 1024 * 1024
         ),
         name="decode",
     )(
@@ -659,19 +741,18 @@
         w_down[0],
     )
     page_pool, mixed = pl.pallas_call(
-        place_kernel,
+        finish_kernel,
         out_shape=(
             jax.ShapeDtypeStruct((SLOTS_DEV, PAGE, 2 * HD), BF16),
             jax.ShapeDtypeStruct((2, REQS, 32), BF16),
         ),
-        in_specs=[smem, vmem, vmem],
-        out_specs=(hbm, vmem),
-        scratch_shapes=[pltpu.SemaphoreType.DMA],
+        in_specs=[vmem, vmem],
+        out_specs=(hbm, hbm),
+        scratch_shapes=[pltpu.SemaphoreType.DMA((7,))],
         compiler_params=pltpu.CompilerParams(vmem_limit_bytes=1024 * 1024),
-        name="place",
+        name="finish",
     )(
-        chosen,
-        pltpu.with_memory_space_constraint(arrived, pltpu.VMEM),
+        pltpu.with_memory_space_constraint(page_pool, pltpu.VMEM),
         pltpu.with_memory_space_constraint(mixed, pltpu.VMEM),
     )
     return (page_pool[None], mixed)

time: 78.9 us -> 75.7 us (0.959)
  Pallas kernels: 78.1 us -> 74.9 us
    pallas_call x2, Pallas kernels: 78.1 us -> 74.9 us  [the longest x1 73.2 us: body(): pl.pallas_call(decode_kernel, out_shape=(pltpu.VMEM((SLOTS_DEV, PAGE, 2 *...]
where the time goes in v3:
time: 75.7 us; the launch traced here: 75.5 us
  Pallas kernels  74.9 us (99%)
    pallas_call x1, Pallas kernels, body(): pl.pallas_call(decode_kernel, out_shape=(pltpu.VMEM((SLOTS_DEV, PAGE, 2 *...  73.2 us
    pallas_call x1, Pallas kernels, body(): pl.pallas_call(finish_kernel, out_shape=(jax.ShapeDtypeStruct((SLOTS_DEV,...  1.72 us

profile of v3, /device:TPU:1, one launch (start us, length us, event | category | flops | bytes accessed | tf_op | source)
XLA Modules:
  0.0 75.5 jit_solution(8769224959870279869)
XLA Ops:
  0.6 73.2 %decode.1 = (bf16[96,64,256]{2,1,0:T(8,128)(2,1)S(1)}, bf16[2,16,32]{2,1,0:T(8,128)(2,1)S(1)}) custom-call(s32[16]{0:T(128)} %lengths_hbm.1, s32[1536]{0:T(1024)} %page_owner_hbm.1, s32[1536]{0:T(1024)} %page_index_hbm.1, s32[1536]{0:T(1024)} %page_dest_hbm.1, s32[12,128]{1,0:T(8,128)} %bitcast.16, bf16[12,8,64,256]{3,2,1,0:T(8,128)(2,1)} %src_hbm.1, ...), custom_call_target="tpu_custom_call" | custom-call | tf_op jit(solution)/shard_map/decode/pallas_call | solution.py:670
  73.8 1.7 %finish.1 = (bf16[96,64,256]{2,1,0:T(8,128)(2,1)}, bf16[2,16,32]{2,1,0:T(8,128)(2,1)}) custom-call(bf16[96,64,256]{2,1,0:T(8,128)(2,1)S(1)} %get-tuple-element.6.pool, bf16[2,16,32]{2,1,0:T(8,128)(2,1)S(1)} %get-tuple-element.7.mixed), custom_call_target="tpu_custom_call" | custom-call | tf_op jit(solution)/shard_map/finish/pallas_call | solution.py:743

commit v4 on v3

--- a/solution.py
+++ b/solution.py
@@ -32,7 +32,7 @@
 F32 = jnp.float32
 N_PLANE = 4
 PACED = 4
-BULK_STARTS = ((14, 0), (14, 1), (14, 1), (5, 0), (14, 1), (4, 0), (28, 0), (34, 0))
+BULK_STARTS = ((16, 0), (12, 1), (12, 1), (5, 0), (12, 1), (4, 0), (28, 0), (38, 0))
 MERGE, GATHER_A, FORWARD_A, GATHER_B, FORWARD_B, PAIR_SUMS, SUMS, BULK = range(4, 12)
 
 
@@ -124,6 +124,8 @@
     ag2_send,
     ag2_recv,
     features,
+    all_router,
+    all_gain,
     rs2_out,
     rs2_pair,
     rs2_send,
@@ -275,8 +277,9 @@
         )
 
     @jax.named_scope("bulk")
-    def start_bulk(point):
+    def start_bulk(point, begin=0, end=None):
         count, window = BULK_STARTS[point]
+        count = (count if end is None else end) - begin
         for i in range(started[0], started[0] + count):
             sem = PACED + point
             if window:
@@ -317,6 +320,24 @@
     arrived[me] = packed[seq * 2 + lax.rem(head, 2), head // 2]
     start_bulk(0)
 
+    tile_row, tile_lane = iota((8, HD), 0), iota((8, HD), 1)
+
+    def to_lanes(block, first):
+        shifted = jnp.where(iota((32, HD), 1) == iota((32, HD), 0) + first, 1.0, 0.0)
+        return dot(block, shifted.astype(BF16))
+
+    own_gain = jnp.where(iota((8, 32), 0) == 0, gain[...].astype(F32), 0.0).astype(BF16)
+    own_extra = to_lanes(own_gain, 32) + to_lanes(router[...], 64)
+    extras = [own_extra]
+
+    def chip_extra():
+        pair = rs1_pair[zs[0], 0].astype(F32)[8:]
+        gains = jnp.where(
+            (tile_lane >= 32) & (tile_lane < 64) & (tile_row == 1), pltpu.roll(pair, 1, 0), 0.0
+        )
+        routers = jnp.where(tile_lane >= 96, pltpu.roll(pair, 32, 1), 0.0)
+        return own_extra + gains + routers
+
     @jax.named_scope("attend")
     def attend_head(t):
         k = kv_heads[t]
@@ -342,11 +363,13 @@
         if t >= N_PLANE:
             pair = rs1_pair.at[zs[t - N_PLANE]]
             arrive(pair, t - N_PLANE)
+            if t == N_PLANE:
+                extras[0] = chip_extra()
             pair = pair[...].astype(F32)
             pair_out = pair[:, :8].reshape(4 * ROWS, HD)
             pair_stats = pair[:, 8:].reshape(4 * ROWS, HD)
             pair_shift = pair_stats[:, :1]
-            pair_total = pair_stats[:, 32:33] + pair_stats[:, 64:65]
+            pair_total = pair_stats[:, 8:9] + pair_stats[:, 16:17]
             joint = jnp.maximum(shift, pair_shift)
             factor, pair_factor = jnp.exp(shift - joint), jnp.exp(pair_shift - joint)
             total = total * factor + pair_total * pair_factor
@@ -354,8 +377,10 @@
             shift = joint
         total_high = total.astype(BF16).astype(F32)
         stats = jnp.where(
-            lane128 < 32, shift, jnp.where(lane128 < 64, total_high, total - total_high)
-        )
+            lane128 < 8, shift, jnp.where(lane128 < 16, total_high, total - total_high)
+        )
+        extra = jnp.broadcast_to(extras[0][None], (16, 8, HD)).reshape(4 * ROWS, HD)
+        stats = jnp.where(lane128 < 32, stats, extra)
         rs1_send[k] = jnp.concatenate(
             [weighted.reshape(16, 8, HD), stats.reshape(16, 8, HD)], axis=1
         ).astype(BF16)
@@ -372,7 +397,7 @@
                 remote(part, rs1_recv.at[slot], MERGE, kv_heads[t], heads[u]).start()
             else:
                 rs1_recv[slot] = part[...]
-    start_bulk(1)
+    start_bulk(1, 0, PACED)
 
     slot_row, slot_lane = iota((HD, HD), 0), iota((HD, HD), 1)
     wanted_slot = slot_row + lax.rem(head, 2) * SLOTS + seq * SLOTS_DEV
@@ -409,6 +434,7 @@
     for u in range(2):
         score = jnp.sum(query * own_fresh[u][:, :HD], axis=1, keepdims=True) * SCALE
         fresh_scores.append(score if u == 0 else jnp.where(later, score, NEG_FILL))
+    start_bulk(1, PACED)
     arrive(rs1_recv.at[pl.ds(0, N_DEV // 2 - 1)], MERGE)
     received = rs1_recv[...].astype(F32)
     outs, stats = received[:, :8], received[:, 8:]
@@ -417,7 +443,7 @@
     factor = jnp.exp(stats[:, :, :1] - top[None])
     weighted = jnp.sum(outs * factor, axis=0)
     totals = jnp.sum(stats * factor, axis=0)
-    total = totals[:, 32:33] + totals[:, 64:65]
+    total = totals[:, 8:9] + totals[:, 16:17]
     for u in range(2):
         weight = jnp.exp(fresh_scores[u] - top)
         total = total + weight
@@ -434,16 +460,46 @@
         )
 
     gather(ag1_send, ag1_recv, GATHER_A)
-    start_bulk(2)
+    start_bulk(2, 0, PACED)
 
     select = [
         jnp.where(iota((32, HD), 1) == iota((32, HD), 0) + q * 32, 1.0, 0.0) for q in range(4)
     ]
-    router_row = iota((ROWS, EXPERTS), 0)
-    wide_router = dot(
-        jnp.where(lax.rem(router_row, 16) == iota((ROWS, EXPERTS), 1) + 1, 1.0, 0.0).astype(BF16),
-        router[...],
-    )
+    extra_blocks = stats.reshape(16, 4, 8, HD)
+    move_row, move_lane = iota((HD, HD), 0), iota((HD, HD), 1)
+
+    def in_order(first):
+        return sum(
+            dot(
+                extra_blocks[:, j].reshape(HD, HD).astype(BF16),
+                jnp.where(
+                    (move_row - first == move_lane - j * 32)
+                    & (move_lane >= j * 32)
+                    & (move_lane < j * 32 + 32),
+                    1.0,
+                    0.0,
+                ).astype(BF16),
+            )
+            for j in range(4)
+        )
+
+    gains, own_routers, other_routers = in_order(32), in_order(64), in_order(96)
+    first_core = core == 0
+    for n in range(N_PLANE * 4):
+        rows = slice(n * 8, n * 8 + 8)
+        routers = (
+            jnp.where(first_core, own_routers[rows], other_routers[rows]),
+            jnp.where(first_core, other_routers[rows], own_routers[rows]),
+        )
+        pair_gains = gains[rows]
+        both = (
+            jnp.where(first_core, pair_gains[0:1], pair_gains[1:2]),
+            jnp.where(first_core, pair_gains[1:2], pair_gains[0:1]),
+        )
+        for c in range(2):
+            place = n // 4 * 8 + c * 4 + n % 4
+            all_router[:, place * HD : (place + 1) * HD] = routers[c].astype(BF16)
+            all_gain[:, place * HD : (place + 1) * HD] = 1.0 / both[c]
     weight_copies[0].wait()
     def forward(whole, phase, point):
         half = whole.at[core]
@@ -452,6 +508,7 @@
         start_bulk(point)
         arrive(half, phase + 1)
 
+    start_bulk(2, PACED)
     forward(ag1_recv, GATHER_A, 3)
     for n in range(N_PLANE):
         for c in range(2):
@@ -463,18 +520,6 @@
         attended[...], wo[...], (((1,), (1,)), ((), ())), preferred_element_type=F32
     )
     scaled = middle * gain[...].astype(F32)
-    lane32 = iota((ROWS, 32), 1)
-    sums = lax.dot_general(
-        scaled,
-        wide_router,
-        (((1,), (1,)), ((), ())),
-        preferred_element_type=F32,
-        precision=HIGHEST,
-    )
-    square = jnp.sum(middle * middle, axis=1, keepdims=True)
-    sums = jnp.where((lane32 == 0) | (lane32 == 16), square, sums)
-    sums_high = sums.astype(BF16).astype(F32)
-    sums = jnp.where(lane32 < 16, sums_high, sums - sums_high)
 
     def packed_rows(block, precision=None):
         return sum(
@@ -482,13 +527,11 @@
             for q in range(4)
         )
 
-    part = jnp.concatenate(
-        [packed_rows(scaled.astype(BF16)), packed_rows(sums.astype(BF16))], axis=0
-    ).astype(BF16)
+    part = packed_rows(scaled.astype(BF16)).astype(BF16)
     ag2_send[...] = part
     ag2_recv[core, slot] = part
     gather(ag2_send, ag2_recv, GATHER_B)
-    start_bulk(4)
+    start_bulk(4, 0, PACED)
     middle_packed = packed_rows(middle, HIGHEST)
 
     spread_row, spread_col = iota((HD, 512), 0), iota((HD, 512), 1)
@@ -500,10 +543,11 @@
     spreads = [spread(j) for j in range(4)]
     for copy in weight_copies[1:]:
         copy.wait()
+    start_bulk(4, PACED)
     forward(ag2_recv, GATHER_B, 5)
     start_bulk(6)
     received = ag2_recv[...].astype(F32)
-    blocks = received[:, :, :8].reshape(32, 4, 8, HD)
+    blocks = received.reshape(32, 4, 8, HD)
     ordered = sum(
         dot(blocks[:, j].reshape(256, HD).astype(BF16), spreads[j]) for j in range(4)
     )
@@ -512,23 +556,13 @@
         features[:, place * HD : (place + 1) * HD] = jnp.concatenate(
             [ordered[n * 8 : n * 8 + 8, q * HD : (q + 1) * HD] for q in range(4)], axis=0
         ).astype(BF16)
-    sums = jnp.sum(jnp.sum(received[:, :, 8:], axis=1), axis=0)
-    fold_row, fold_col = iota((HD, HD), 0), iota((HD, HD), 1)
-    folded = jnp.concatenate(
-        [
-            dot(
-                sums,
-                jnp.where(
-                    (fold_row // 32 == q) & (lax.rem(fold_row, 16) == fold_col), 1.0, 0.0
-                ),
-                HIGHEST,
-            )
-            for q in range(4)
-        ],
-        axis=0,
+    whole = features[...]
+    unscaled = whole.astype(F32) * all_gain[...]
+    squares = jnp.sum(unscaled * unscaled, axis=1, keepdims=True)
+    inverse_rms = lax.rsqrt(squares / D + EPSILON)
+    logits = inverse_rms * lax.dot_general(
+        whole, all_router[...], (((1,), (1,)), ((), ())), preferred_element_type=F32
     )
-    inverse_rms = lax.rsqrt(folded[:, :1] / D + EPSILON)
-    logits = folded * inverse_rms
     diagonal = iota((REQS, REQS), 0) == iota((REQS, REQS), 1)
 
     def picked(choice):
@@ -543,7 +577,7 @@
         return jnp.concatenate(rows, axis=0).astype(jnp.int32)
 
     first, second = picked(0), picked(1)
-    expert_lane = iota((ROWS, HD), 1) - 1
+    expert_lane = iota((ROWS, EXPERTS), 1)
     first_logit = jnp.sum(jnp.where(expert_lane == first, logits, 0.0), axis=1, keepdims=True)
     second_logit = jnp.sum(jnp.where(expert_lane == second, logits, 0.0), axis=1, keepdims=True)
     share = jnp.where(
@@ -702,9 +736,11 @@
             pltpu.VMEM((8, HD), BF16),
             pltpu.VMEM((2, N_DEV // 2, 8, HD), BF16),
             pltpu.VMEM((ROWS, D), BF16),
-            pltpu.VMEM((16, HD), BF16),
-            pltpu.VMEM((2, N_DEV // 2, 16, HD), BF16),
+            pltpu.VMEM((8, HD), BF16),
+            pltpu.VMEM((2, N_DEV // 2, 8, HD), BF16),
             pltpu.VMEM((ROWS, D), BF16),
+            pltpu.VMEM((EXPERTS, D), BF16),
+            pltpu.VMEM((1, D), F32),
             pltpu.VMEM((16, 4, 8, HD), BF16),
             pltpu.VMEM((16, 4, 8, HD), BF16),
             pltpu.VMEM((16, 4, 8, HD), BF16),

time: 75.7 us -> 75.4 us (level)
  no operation moved by 1% of the time
where the time goes in v4:
time: 75.4 us; the launch traced here: 75.3 us
  Pallas kernels  74.6 us (99%)
    pallas_call x1, Pallas kernels, body(): pl.pallas_call(decode_kernel, out_shape=(pltpu.VMEM((SLOTS_DEV, PAGE, 2 *...  72.9 us
    pallas_call x1, Pallas kernels, body(): pl.pallas_call(finish_kernel, out_shape=(jax.ShapeDtypeStruct((SLOTS_DEV,...  1.72 us

profile of v4, /device:TPU:1, one launch (start us, length us, event | category | flops | bytes accessed | tf_op | source)
XLA Modules:
  0.0 75.3 jit_solution(15766830288040995082)
XLA Ops:
  0.6 72.9 %decode.1 = (bf16[96,64,256]{2,1,0:T(8,128)(2,1)S(1)}, bf16[2,16,32]{2,1,0:T(8,128)(2,1)S(1)}) custom-call(s32[16]{0:T(128)} %lengths_hbm.1, s32[1536]{0:T(1024)} %page_owner_hbm.1, s32[1536]{0:T(1024)} %page_index_hbm.1, s32[1536]{0:T(1024)} %page_dest_hbm.1, s32[12,128]{1,0:T(8,128)} %bitcast.16, bf16[12,8,64,256]{3,2,1,0:T(8,128)(2,1)} %src_hbm.1, ...), custom_call_target="tpu_custom_call" | custom-call | tf_op jit(solution)/shard_map/decode/pallas_call | solution.py:704
  73.5 1.7 %finish.1 = (bf16[96,64,256]{2,1,0:T(8,128)(2,1)}, bf16[2,16,32]{2,1,0:T(8,128)(2,1)}) custom-call(bf16[96,64,256]{2,1,0:T(8,128)(2,1)S(1)} %get-tuple-element.6.pool, bf16[2,16,32]{2,1,0:T(8,128)(2,1)S(1)} %get-tuple-element.7.mixed), custom_call_target="tpu_custom_call" | custom-call | tf_op jit(solution)/shard_map/finish/pallas_call | solution.py:779
